TPU v7x, 32 devices: a whole 2x2x4 slice. The times are simulated.
32 devices in a mesh: bias: 2 (over x), ea: 16 (over z, y, core).
Axes of the slice: x: 2, y: 2, z: 4, core: 2. Of those that a mesh axis runs over, the one named last changes fastest.
Arguments:
- g_lesser: bfloat16 [512, 2, 256, 256], P(('bias', 'ea')), parts along dimension 0, may hold values from -6 to 6
- g_greater: bfloat16 [512, 2, 256, 256], P(('bias', 'ea')), parts along dimension 0, may hold values from -6 to 6
- g_free: bfloat16 [512, 2, 256, 256], P(('bias', 'ea')), parts along dimension 0, may hold values from -3 to 3
- coulomb: bfloat16 [256, 256], replicated, may hold values from -0.375 to 0.375
Outputs:
- g_new: bfloat16 [512, 2, 256, 256], P(('bias', 'ea')), parts along dimension 0
There are 2 independent parts, one for each index of `bias`. A program takes and returns all parts, laid end to end along the dimension named above; an argument that names none is the same for every part. Nothing has to cross between parts.
All inputs are finite; a program needn't handle non-finite values.
Results may differ from a plain program's by a relative error of at most 0.022.
Values may be sent and summed in bfloat16 or wider, within the bound.
A program may use at most 192 MiB of HBM per device.

v0:
```python
import functools
import math

import jax
import jax.numpy as jnp
import numpy as np
from jax import lax
from jax.experimental import pallas as pl
from jax.experimental.pallas import tpu as pltpu
from jax.sharding import PartitionSpec as P

NE = 256


def dft_tables(length, count):
    freq = jnp.arange(length, dtype=jnp.int32)
    places = jnp.arange(count, dtype=jnp.int32)
    phase = freq[:, None] * places[None, :] % length
    angle = phase.astype(jnp.float32) * (2.0 * math.pi / length)
    cosine = jnp.cos(angle)
    sine = jnp.sin(angle)
    stacked = jnp.concatenate([cosine, sine], axis=0)
    upper = stacked.astype(jnp.bfloat16)
    lower = (stacked - upper.astype(jnp.float32)).astype(jnp.bfloat16)
    backward = jnp.concatenate([cosine.T, sine.T], axis=0)
    return (upper, lower, backward)


def forward(tables, block, sign):
    upper, lower = tables
    length = upper.shape[0] // 2
    real_part = block[:, 0].reshape(block.shape[0], -1)
    imag_part = block[:, 1].reshape(block.shape[0], -1)
    width = real_part.shape[1]
    joined = jnp.concatenate([real_part, imag_part], axis=1)
    result = jnp.dot(upper, joined, preferred_element_type=jnp.float32)
    result = result + jnp.dot(lower, joined, preferred_element_type=jnp.float32)
    cos_real = result[:length, :width]
    cos_imag = result[:length, width:]
    sin_real = result[length:, :width]
    sin_imag = result[length:, width:]
    return (cos_real - sign * sin_imag, cos_imag + sign * sin_real)


def inverse(backward, real_part, imag_part, scale):
    count = backward.shape[0] // 2
    width = real_part.shape[1]
    joined = jnp.concatenate([real_part, imag_part], axis=1)
    result = jnp.dot(
        backward, joined, precision=lax.Precision.HIGH, preferred_element_type=jnp.float32
    )
    cos_real = result[:count, :width]
    cos_imag = result[:count, width:]
    sin_real = result[count:, :width]
    sin_imag = result[count:, width:]
    return ((cos_real - sin_imag) * scale, (cos_imag + sin_real) * scale)


def complex_mul(left, right):
    return (left[0] * right[0] - left[1] * right[1], left[0] * right[1] + left[1] * right[0])


def restack(real_part, imag_part, shape):
    return jnp.stack([real_part.reshape(shape), imag_part.reshape(shape)], axis=1).astype(
        jnp.bfloat16
    )


def batched(left, right):
    return jnp.einsum("eij,ejk->eik", left, right, preferred_element_type=jnp.float32)


def dyson(sigma_real, sigma_imag, g_free):
    free_real = g_free[:, 0]
    free_imag = g_free[:, 1]
    right_real = (batched(sigma_real, free_real) - batched(sigma_imag, free_imag)).astype(
        jnp.bfloat16
    )
    right_imag = (batched(sigma_real, free_imag) + batched(sigma_imag, free_real)).astype(
        jnp.bfloat16
    )
    out_real = (
        free_real.astype(jnp.float32)
        + batched(free_real, right_real)
        - batched(free_imag, right_imag)
    )
    out_imag = (
        free_imag.astype(jnp.float32)
        + batched(free_real, right_imag)
        + batched(free_imag, right_real)
    )
    return jnp.stack([out_real, out_imag], axis=1).astype(jnp.bfloat16)


def plain(g_lesser, g_greater, g_free, coulomb):
    length = 2 * NE
    upper, lower, backward = dft_tables(length, NE)
    tables = (upper, lower)
    scale = 1.0 / (length * NE)
    greater_t = jnp.swapaxes(g_greater, 2, 3)
    lesser_rows, greater_rows = (
        lax.all_to_all(g_lesser, "ea", split_axis=2, concat_axis=0, tiled=True),
        lax.all_to_all(greater_t, "ea", split_axis=2, concat_axis=0, tiled=True),
    )
    spec_lesser = forward(tables, lesser_rows, -1.0)
    element_shape = (NE, lesser_rows.shape[2], lesser_rows.shape[3])
    spec_greater = forward(tables, greater_rows, 1.0)
    joined = complex_mul(spec_lesser, spec_greater)
    polar_real, polar_imag = inverse(backward, joined[0], joined[1], scale)
    polar_rows = restack(polar_real, polar_imag, element_shape)
    polar = lax.all_to_all(polar_rows, "ea", split_axis=0, concat_axis=2, tiled=True)
    mixed_real = jnp.einsum(
        "eij,jk->eik", polar[:, 0], coulomb, preferred_element_type=jnp.float32
    ).astype(jnp.bfloat16)
    mixed_imag = jnp.einsum(
        "eij,jk->eik", polar[:, 1], coulomb, preferred_element_type=jnp.float32
    ).astype(jnp.bfloat16)
    square_real = batched(mixed_real, mixed_real) - batched(mixed_imag, mixed_imag)
    square_imag = batched(mixed_real, mixed_imag) + batched(mixed_imag, mixed_real)
    inner_real = (mixed_real.astype(jnp.float32) + square_real).astype(jnp.bfloat16)
    inner_imag = (mixed_imag.astype(jnp.float32) + square_imag).astype(jnp.bfloat16)
    screen_real = coulomb.astype(jnp.float32)[None] + jnp.einsum(
        "ij,ejk->eik", coulomb, inner_real, preferred_element_type=jnp.float32
    )
    screen_imag = jnp.einsum("ij,ejk->eik", coulomb, inner_imag, preferred_element_type=jnp.float32)
    screen = jnp.stack([screen_real, screen_imag], axis=1).astype(jnp.bfloat16)
    screen_rows = lax.all_to_all(screen, "ea", split_axis=2, concat_axis=0, tiled=True)
    spec_screen = forward(tables, screen_rows, -1.0)
    folded = complex_mul(spec_lesser, spec_screen)
    sigma_real, sigma_imag = inverse(backward, folded[0], folded[1], scale)
    sigma_rows = restack(sigma_real, sigma_imag, element_shape)
    sigma = lax.all_to_all(sigma_rows, "ea", split_axis=0, concat_axis=2, tiled=True)
    return dyson(sigma[:, 0], sigma[:, 1], g_free)


MESH = pl.DeviceIdType.MESH
CHUNKS = 4
LANES = 128
VMEM_BYTES = 60 * 1024 * 1024


def transform_table(count):
    length = 2 * count
    phase = np.arange(length)[:, None] * np.arange(count)[None, :] % length
    angle = phase * (2.0 * math.pi / length)
    cosine, sine = np.cos(angle), np.sin(angle)
    return np.block([[cosine, sine], [-sine, cosine]]).astype(np.float32)


def greet(n):
    me = lax.axis_index("ea")
    barrier = pltpu.get_barrier_semaphore()

    def hello(k, carry):
        pl.semaphore_signal(
            barrier, inc=1, device_id={"ea": lax.rem(me + k, n)}, device_id_type=MESH
        )
        return carry

    lax.fori_loop(1, n, hello, 0)
    pl.semaphore_wait(barrier, n - 1)


def exchange_kernel(
    n, count, first, scale, *refs
):
    if first:
        (lesser, other, table, table_t, volts, out, kept,
         lesser_buf, other_buf, folded, in_send, in_recv, out_send, out_recv, own_in, own_out, keep,
         lesser_raw, other_raw, lesser_rows, other_rows) = refs
        streams = ((lesser_rows, lesser_buf), (other_rows, other_buf))
    else:
        (kept, other, table, table_t, out,
         lesser_buf, other_buf, folded, in_send, in_recv, out_send, out_recv, own_in, own_out, keep) = refs
        streams = ((other, other_buf),)
    me = lax.axis_index("ea")
    rows = folded.shape[1]
    each = count // n
    group = rows // CHUNKS

    def incoming(s, q, k):
        peer = lax.rem(me + k, n)
        source, target = streams[s]
        return pltpu.make_async_remote_copy(
            src_ref=source.at[:, pl.ds(peer * rows + q * group, group)],
            dst_ref=target.at[:, pl.ds(q * group, group), pl.ds(me * each, each)],
            send_sem=in_send.at[s, q, k],
            recv_sem=in_recv.at[s, q, k],
            device_id={"ea": peer},
            device_id_type=MESH,
        )

    def outgoing(q, k):
        peer = lax.rem(me + k, n)
        return pltpu.make_async_remote_copy(
            src_ref=folded.at[:, pl.ds(q * group, group), pl.ds(peer * each, each)],
            dst_ref=out.at[:, pl.ds(me * rows + q * group, group)],
            send_sem=out_send.at[q, k],
            recv_sem=out_recv.at[q, k],
            device_id={"ea": peer},
            device_id_type=MESH,
        )

    def own_incoming(s):
        source, target = streams[s]
        return pltpu.make_async_copy(
            source.at[:, pl.ds(me * rows, rows)],
            target.at[:, :, pl.ds(me * each, each)],
            own_in.at[s],
        )

    def send_chunk(s, q):
        def send_one(k, inner):
            incoming(s, q, k).start()
            return inner

        lax.fori_loop(1, n, send_one, 0)

    if first:
        raw = (
            pltpu.make_async_copy(lesser, lesser_raw, own_in.at[0]),
            pltpu.make_async_copy(other, other_raw, own_in.at[1]),
        )
        for copy in raw:
            copy.start()
        greet(n)
        raw[0].wait()
        mine = pl.ds(pl.multiple_of(me * each, each), each)

        def regroup(k, carry):
            peer = lax.rem(me + k, n)
            block = pl.ds(pl.multiple_of(peer * rows, rows), rows)
            for c in range(2):
                lesser_rows[c, block] = jnp.swapaxes(lesser_raw[:, c, block, :], 0, 1)
            return carry

        def regroup_and_send(k, carry):
            regroup(k, carry)

            def send_one(q, inner):
                incoming(0, q, k).start()
                return inner

            return lax.fori_loop(0, CHUNKS, send_one, carry)

        lax.fori_loop(1, n, regroup_and_send, 0)
        regroup(0, 0)
        raw[1].wait()
        for low in range(0, rows * n, LANES):
            for c in range(2):
                turned = jnp.stack(
                    [other_raw[e, c, :, low : low + LANES].T for e in range(each)], axis=0
                )
                other_rows[c, low : low + LANES] = jnp.swapaxes(turned, 0, 1)
        lax.fori_loop(0, CHUNKS, lambda q, carry: (send_chunk(1, q), carry)[1], 0)
        for source, target in streams:
            for c in range(2):
                target[c, :, mine, :] = source[c, pl.ds(me * rows, rows)]
    else:
        pltpu.make_async_copy(kept, lesser_buf, keep).start()
        own_incoming(0).start()
        greet(n)
        lax.fori_loop(0, CHUNKS, lambda q, carry: (send_chunk(0, q), carry)[1], 0)
        own_incoming(0).wait()
        pltpu.make_async_copy(kept, lesser_buf, keep).wait()

    length = 2 * count

    def fold(row, carry):
        left = jnp.concatenate([lesser_buf[0, row], lesser_buf[1, row]], axis=0)
        imag = other_buf[1, row]
        right = jnp.concatenate([other_buf[0, row], -imag if first else imag], axis=0)
        left_spec = jnp.dot(table[...], left, preferred_element_type=jnp.float32)
        right_spec = jnp.dot(table[...], right, preferred_element_type=jnp.float32)
        left_real, left_imag = left_spec[:length], left_spec[length:]
        right_real, right_imag = right_spec[:length], right_spec[length:]
        if first:
            real = left_real * right_real + left_imag * right_imag
            imag = left_imag * right_real - left_real * right_imag
        else:
            real = left_real * right_real - left_imag * right_imag
            imag = left_real * right_imag + left_imag * right_real
        product = jnp.concatenate([real, imag], axis=0).astype(jnp.bfloat16)
        result = jnp.dot(table_t[...], product, preferred_element_type=jnp.float32) * scale
        result = result.astype(jnp.bfloat16)
        if first:
            result = jnp.dot(result, volts[...], preferred_element_type=jnp.float32)
            result = result.astype(jnp.bfloat16)
        folded[0, row] = result[:count]
        folded[1, row] = result[count:]
        return carry

    def work(q, carry):
        for s in range(len(streams)):
            def wait_one(k, inner):
                incoming(s, q, k).wait()
                return inner
            lax.fori_loop(1, n, wait_one, 0)
        lax.fori_loop(q * group, (q + 1) * group, fold, 0)

        def send_one(k, inner):
            outgoing(q, k).start()
            return inner

        lax.fori_loop(1, n, send_one, 0)
        return carry

    lax.fori_loop(0, CHUNKS, work, 0)
    own_result = pltpu.make_async_copy(
        folded.at[:, :, pl.ds(me * each, each)], out.at[:, pl.ds(me * rows, rows)], own_out
    )
    own_result.start()
    if first:
        keeping = pltpu.make_async_copy(lesser_buf, kept, keep)
        keeping.start()

    def finish(q, carry):
        def wait_one(k, inner):
            outgoing(q, k).wait()
            return inner
        return lax.fori_loop(1, n, wait_one, carry)

    lax.fori_loop(0, CHUNKS, finish, 0)
    own_result.wait()
    if first:
        keeping.wait()


def exchange(n, count, first, scale, operands):
    orbitals, width = operands[1].shape[-3 if not first else -2], operands[1].shape[-1]
    each = count // n
    rows = orbitals // n
    hbm = pl.BlockSpec(memory_space=pl.ANY)
    vmem = pl.BlockSpec(memory_space=pltpu.VMEM)
    streams = 2 if first else 1
    out_shape = [jax.ShapeDtypeStruct((2, orbitals, each, width), jnp.bfloat16)]
    if first:
        out_shape.append(jax.ShapeDtypeStruct((2, rows, count, width), jnp.bfloat16))
    buffer = pltpu.VMEM((2, rows, count, width), jnp.bfloat16)
    dma = pltpu.SemaphoreType.DMA
    staging = []
    if first:
        staging = [pltpu.VMEM((each, 2, orbitals, width), jnp.bfloat16)] * 2
        staging += [pltpu.VMEM((2, orbitals, each, width), jnp.bfloat16)] * 2
    return pl.pallas_call(
        functools.partial(exchange_kernel, n, count, first, scale),
        name="polarize" if first else "dress",
        out_shape=out_shape,
        in_specs=[hbm, hbm] + [vmem] * (len(operands) - 2),
        out_specs=[hbm] * len(out_shape),
        scratch_shapes=[
            buffer, buffer, buffer,
            dma((streams, CHUNKS, n)), dma((streams, CHUNKS, n)),
            dma((CHUNKS, n)), dma((CHUNKS, n)),
            dma((streams,)), dma, dma,
        ] + staging,
        compiler_params=pltpu.CompilerParams(
            collective_id=0 if first else 1, has_side_effects=True, vmem_limit_bytes=VMEM_BYTES
        ),
    )(*operands)


def dot(left, right):
    return jnp.dot(left, right, preferred_element_type=jnp.float32)


def screen_kernel(mixed, volts, out):
    bare = volts[...]
    for e in range(mixed.shape[0]):
        real, imag = mixed[e, 0], mixed[e, 1]
        square_real = dot(real, real) - dot(imag, imag)
        square_imag = dot(real, imag) + dot(imag, real)
        inner_real = (real.astype(jnp.float32) + square_real).astype(jnp.bfloat16)
        inner_imag = (imag.astype(jnp.float32) + square_imag).astype(jnp.bfloat16)
        out[e, 0] = (bare.astype(jnp.float32) + dot(bare, inner_real)).astype(jnp.bfloat16)
        out[e, 1] = dot(bare, inner_imag).astype(jnp.bfloat16)


def dyson_kernel(sigma, free, out):
    for e in range(sigma.shape[0]):
        real, imag = sigma[e, 0], sigma[e, 1]
        free_real, free_imag = free[e, 0], free[e, 1]
        right_real = (dot(real, free_real) - dot(imag, free_imag)).astype(jnp.bfloat16)
        right_imag = (dot(real, free_imag) + dot(imag, free_real)).astype(jnp.bfloat16)
        out_real = dot(free_real, right_real) - dot(free_imag, right_imag)
        out_imag = dot(free_real, right_imag) + dot(free_imag, right_real)
        out[e, 0] = (free_real.astype(jnp.float32) + out_real).astype(jnp.bfloat16)
        out[e, 1] = (free_imag.astype(jnp.float32) + out_imag).astype(jnp.bfloat16)


def per_energy(kernel, name, matrices, others):
    each, two, rows, width = matrices.shape
    block = pl.BlockSpec((2, two, rows, width), lambda i: (i, 0, 0, 0))
    specs = [block if other.ndim == 4 else pl.BlockSpec(memory_space=pltpu.VMEM) for other in others]
    products = 6 if name == "screen" else 8
    return pl.pallas_call(
        kernel,
        name=name,
        grid=(each // 2,),
        out_shape=jax.ShapeDtypeStruct(matrices.shape, jnp.bfloat16),
        in_specs=[block] + specs,
        out_specs=block,
        cost_estimate=pl.CostEstimate(
            flops=2 * products * each * rows * rows * width,
            bytes_accessed=4 * two * each * rows * width,
            transcendentals=0,
        ),
    )(matrices, *others)


def per_device(n, g_lesser, g_greater, g_free, coulomb):
    each, _, orbitals, _ = g_lesser.shape
    count = n * each
    if each % 16 or orbitals % (n * 16) or orbitals % LANES:
        return plain(g_lesser, g_greater, g_free, coulomb)
    scale = 1.0 / (2 * count * count)
    full = transform_table(count)
    table = jnp.asarray(full).astype(jnp.bfloat16)
    table_t = jnp.asarray(full.T).astype(jnp.bfloat16)
    mixed, kept = exchange(n, count, True, scale, (g_lesser, g_greater, table, table_t, coulomb))
    mixed = jnp.transpose(mixed, (2, 0, 1, 3))
    screen = per_energy(screen_kernel, "screen", mixed, (coulomb,))
    screen = jnp.transpose(screen, (1, 2, 0, 3))
    (sigma,) = exchange(n, count, False, scale, (kept, screen, table, table_t))
    sigma = jnp.transpose(sigma, (2, 0, 1, 3))
    return per_energy(dyson_kernel, "dyson", sigma, (g_free,))


def solution(mesh):
    return jax.shard_map(
        functools.partial(per_device, mesh.shape["ea"]),
        mesh=mesh,
        in_specs=(
            P(("bias", "ea"), None, None, None),
            P(("bias", "ea"), None, None, None),
            P(("bias", "ea"), None, None, None),
            P(),
        ),
        out_specs=P(("bias", "ea"), None, None, None),
        check_vma=False,
    )
```

profile of v0, /device:TPU:15, one launch (start us, length us, event | category | flops | bytes accessed | tf_op | source)
XLA Modules:
  0.0 508.7 jit_solution(4826903949875256365)
XLA Ops:
  0.0 281.9 %polarize.1 = (bf16[2,256,16,256]{3,2,1,0:T(8,128)(2,1)}, bf16[2,16,256,256]{3,2,1,0:T(8,128)(2,1)}) custom-call(bf16[16,2,256,256]{3,2,1,0:T(8,128)(2,1)} %refs_0_.1, bf16[16,2,256,256]{3,2,1,0:T(8,128)(2,1)} %refs_1_.1, bf16[1024,512]{1,0:T(8,128)(2,1)} %constant.9.refs_2_, bf16[512,1024]{1,0:T(8,128)(2,1)} %constant.10.refs_3_, bf16[256,256]{1,0:T(8,128)(2,1)} %volts.1), custom_call_target="tpu_custom_call" | custom-call | tf_op jit(solution)/shard_map/polarize/pallas_call | solution.py:345
  281.9 5.7 %copy.15 = bf16[2,256,16,256]{3,1,0,2:T(8,128)(2,1)} copy(bf16[2,256,16,256]{3,2,1,0:T(8,128)(2,1)} %get-tuple-element.8) | data formatting | bytes 8388608 | tf_op jit(solution)/shard_map/polarize/pallas_call | solution.py:345
  287.6 10.2 %screen.1 = bf16[16,2,256,256]{3,2,1,0:T(8,128)(2,1)} custom-call(bf16[16,2,256,256]{3,2,1,0:T(8,128)(2,1)} %bitcast.10, bf16[256,256]{1,0:T(8,128)(2,1)} %volts.1), custom_call_target="tpu_custom_call" | custom-call | flops 3221225472 | bytes 8388608 | tf_op jit(solution)/shard_map/screen/pallas_call | solution.py:396
  297.8 6.6 %copy.14 = bf16[16,2,256,256]{3,0,2,1:T(8,128)(2,1)} copy(bf16[16,2,256,256]{3,2,1,0:T(8,128)(2,1)} %screen.1) | data formatting | bytes 8388608 | tf_op jit(solution)/shard_map/screen/pallas_call | solution.py:396
  304.4 187.4 %dress.1 = bf16[2,256,16,256]{3,2,1,0:T(8,128)(2,1)} custom-call(bf16[2,16,256,256]{3,2,1,0:T(8,128)(2,1)} %get-tuple-element.7.refs_0_, bf16[2,256,16,256]{3,2,1,0:T(8,128)(2,1)} %bitcast.9, bf16[1024,512]{1,0:T(8,128)(2,1)} %constant.9.refs_2_, bf16[512,1024]{1,0:T(8,128)(2,1)} %constant.10.refs_3_), custom_call_target="tpu_custom_call" | custom-call | tf_op jit(solution)/shard_map/dress/pallas_call | solution.py:345
  491.8 5.6 %copy.13 = bf16[2,256,16,256]{3,1,0,2:T(8,128)(2,1)} copy(bf16[2,256,16,256]{3,2,1,0:T(8,128)(2,1)} %dress.1) | data formatting | bytes 8388608 | tf_op jit(solution)/shard_map/dress/pallas_call | solution.py:345
  497.4 11.3 %dyson.1 = bf16[16,2,256,256]{3,2,1,0:T(8,128)(2,1)} custom-call(bf16[16,2,256,256]{3,2,1,0:T(8,128)(2,1)} %bitcast.11, bf16[16,2,256,256]{3,2,1,0:T(8,128)(2,1)} %free.1), custom_call_target="tpu_custom_call" | custom-call | flops 4294967296 | bytes 8388608 | tf_op jit(solution)/shard_map/dyson/pallas_call | solution.py:396
where the time goes:
time: 509 us
  Pallas kernels  491 us (96%)
  local copies, waits for them, and re-layouts  17.9 us (4%)
    pallas_call x2, Pallas kernels, exchange(): pl.pallas_call(functools.partial(exchange_kernel, n, count, first, scale)...  469 us
    pallas_call x2, Pallas kernels, per_energy(): pl.pallas_call(kernel, name=name, grid=(each // 2,), out_shape=jax.ShapeD...  21.5 us
    pallas_call x2, local copies, waits for them, and re-layouts, exchange(): pl.pallas_call(functools.partial(exchange_kernel, n, count, first, scale)...  11.3 us

commit v1 on v0

--- a/solution.py
+++ b/solution.py
@@ -147,183 +147,330 @@
     return np.block([[cosine, sine], [-sine, cosine]]).astype(np.float32)
 
 
-def greet(n):
-    me = lax.axis_index("ea")
+class Place:
+    def __init__(self, n):
+        self.n = n
+        self.side = n // 2
+        self.plane = lax.axis_index("bias")
+        self.me = lax.axis_index("ea")
+        self.half = lax.div(self.me, self.side)
+        self.seat = lax.rem(self.me, self.side)
+        self.member = self.plane * self.side + self.seat
+
+    def of_member(self, member):
+        return {
+            "bias": lax.div(member, self.side),
+            "ea": self.half * self.side + lax.rem(member, self.side),
+        }
+
+
+def greet(place):
+    n = place.n
     barrier = pltpu.get_barrier_semaphore()
+    mine = place.plane * n + place.me
 
     def hello(k, carry):
+        other = lax.rem(mine + k, 2 * n)
         pl.semaphore_signal(
-            barrier, inc=1, device_id={"ea": lax.rem(me + k, n)}, device_id_type=MESH
+            barrier,
+            inc=1,
+            device_id={"bias": lax.div(other, n), "ea": lax.rem(other, n)},
+            device_id_type=MESH,
         )
         return carry
 
-    lax.fori_loop(1, n, hello, 0)
-    pl.semaphore_wait(barrier, n - 1)
-
-
-def exchange_kernel(
-    n, count, first, scale, *refs
+    lax.fori_loop(1, 2 * n, hello, 0)
+    pl.semaphore_wait(barrier, 2 * n - 1)
+
+
+def loop(low, high, body):
+    def step(k, carry):
+        body(k)
+        return carry
+
+    lax.fori_loop(low, high, step, 0)
+
+
+def fold_row(first, scale, count, table, table_t, lesser_buf, other_buf, folded, volts, row):
+    length = 2 * count
+    left = jnp.concatenate([lesser_buf[0, row], lesser_buf[1, row]], axis=0)
+    imag = other_buf[1, row]
+    right = jnp.concatenate([other_buf[0, row], -imag if first else imag], axis=0)
+    left_spec = jnp.dot(table[...], left, preferred_element_type=jnp.float32)
+    right_spec = jnp.dot(table[...], right, preferred_element_type=jnp.float32)
+    left_real, left_imag = left_spec[:length], left_spec[length:]
+    right_real, right_imag = right_spec[:length], right_spec[length:]
+    if first:
+        real = left_real * right_real + left_imag * right_imag
+        imag = left_imag * right_real - left_real * right_imag
+    else:
+        real = left_real * right_real - left_imag * right_imag
+        imag = left_real * right_imag + left_imag * right_real
+    product = jnp.concatenate([real, imag], axis=0).astype(jnp.bfloat16)
+    result = jnp.dot(table_t[...], product, preferred_element_type=jnp.float32) * scale
+    result = result.astype(jnp.bfloat16)
+    if first:
+        result = jnp.dot(result, volts[...], preferred_element_type=jnp.float32)
+        result = result.astype(jnp.bfloat16)
+    folded[0, row] = result[:count]
+    folded[1, row] = result[count:]
+
+
+def polarize_kernel(
+    n, count, scale, lesser, other, table, table_t, volts, out, kept,
+    lesser_buf, other_buf, folded, in_send, in_recv, out_send, out_recv, own_in, own_out, keep,
+    swap_send, swap_recv, lesser_raw, other_raw, lesser_rows, other_rows,
 ):
-    if first:
-        (lesser, other, table, table_t, volts, out, kept,
-         lesser_buf, other_buf, folded, in_send, in_recv, out_send, out_recv, own_in, own_out, keep,
-         lesser_raw, other_raw, lesser_rows, other_rows) = refs
-        streams = ((lesser_rows, lesser_buf), (other_rows, other_buf))
-    else:
-        (kept, other, table, table_t, out,
-         lesser_buf, other_buf, folded, in_send, in_recv, out_send, out_recv, own_in, own_out, keep) = refs
-        streams = ((other, other_buf),)
-    me = lax.axis_index("ea")
+    place = Place(n)
+    me, plane, half, side = place.me, place.plane, place.half, place.side
     rows = folded.shape[1]
     each = count // n
     group = rows // CHUNKS
+    wide = side * group
+    stages = (lesser_rows, other_rows)
+    targets = (lesser_buf, other_buf)
+
+    def swap(s, q):
+        span = pl.ds(q * wide, wide)
+        return pltpu.make_async_remote_copy(
+            src_ref=stages[s].at[2, :, span],
+            dst_ref=stages[s].at[plane, :, span],
+            send_sem=swap_send.at[s, q],
+            recv_sem=swap_recv.at[s, q],
+            device_id={"bias": 1 - plane},
+            device_id_type=MESH,
+        )
+
+    def ends(s, q, peer):
+        source = stages[s].at[
+            lax.div(peer, side), :, pl.ds(q * wide + lax.rem(peer, side) * group, group)
+        ]
+        target = targets[s].at[:, pl.ds(q * group, group), pl.ds(me * each, each)]
+        return source, target
 
     def incoming(s, q, k):
         peer = lax.rem(me + k, n)
-        source, target = streams[s]
+        source, target = ends(s, q, peer)
         return pltpu.make_async_remote_copy(
-            src_ref=source.at[:, pl.ds(peer * rows + q * group, group)],
-            dst_ref=target.at[:, pl.ds(q * group, group), pl.ds(me * each, each)],
+            src_ref=source,
+            dst_ref=target,
             send_sem=in_send.at[s, q, k],
             recv_sem=in_recv.at[s, q, k],
             device_id={"ea": peer},
             device_id_type=MESH,
         )
 
+    def own_incoming(s, q):
+        source, target = ends(s, q, me)
+        return pltpu.make_async_copy(source, target, own_in.at[s, q])
+
+    def spread(s, q, bias):
+        def send_one(j):
+            peer = bias * side + lax.rem(place.seat + j, side)
+            k = lax.rem(peer - me + n, n)
+
+            @pl.when(k == 0)
+            def _():
+                own_incoming(s, q).start()
+
+            @pl.when(k != 0)
+            def _():
+                incoming(s, q, k).start()
+
+        loop(0, side, send_one)
+
     def outgoing(q, k):
+        peer = lax.rem(place.member + k, n)
+        return pltpu.make_async_remote_copy(
+            src_ref=folded.at[:, pl.ds(q * group, group), pl.ds(peer * each, each)],
+            dst_ref=out.at[:, pl.ds((q * n + place.member) * group, group)],
+            send_sem=out_send.at[q, k],
+            recv_sem=out_recv.at[q, k],
+            device_id=place.of_member(peer),
+            device_id_type=MESH,
+        )
+
+    def own_outgoing(q):
+        return pltpu.make_async_copy(
+            folded.at[:, pl.ds(q * group, group), pl.ds(place.member * each, each)],
+            out.at[:, pl.ds((q * n + place.member) * group, group)],
+            own_out.at[q],
+        )
+
+    raw = (
+        pltpu.make_async_copy(lesser, lesser_raw, keep.at[0]),
+        pltpu.make_async_copy(other, other_raw, keep.at[1]),
+    )
+    for copy in raw:
+        copy.start()
+    greet(place)
+    raw[0].wait()
+
+    def regroup(q):
+        for h in range(2):
+            slot = jnp.where(plane == h, h, 2)
+            block = pl.ds(pl.multiple_of((2 * q + h) * wide, wide), wide)
+            for c in range(2):
+                lesser_rows[slot, c, pl.ds(pl.multiple_of(q * wide, wide), wide)] = jnp.swapaxes(
+                    lesser_raw[:, c, block, :], 0, 1
+                )
+        swap(0, q).start()
+        spread(0, q, plane)
+
+    loop(0, CHUNKS, regroup)
+    raw[1].wait()
+    for low in range(0, rows * n, LANES):
+        for c in range(2):
+            turned = jnp.stack(
+                [other_raw[e, c, :, low : low + LANES].T for e in range(each)], axis=0
+            )
+            turned = jnp.swapaxes(turned, 0, 1)
+            for at in range(0, LANES, wide):
+                piece = (low + at) // wide
+                slot = jnp.where(plane == piece % 2, piece % 2, 2)
+                start = piece // 2 * wide
+                other_rows[slot, c, start : start + wide] = turned[at : at + wide]
+    loop(0, CHUNKS, lambda q: swap(1, q).start())
+
+    def relay(q):
+        swap(0, q).wait_recv()
+        spread(0, q, 1 - plane)
+
+    loop(0, CHUNKS, relay)
+
+    def relay_other(q):
+        spread(1, q, plane)
+        swap(1, q).wait_recv()
+        spread(1, q, 1 - plane)
+
+    loop(0, CHUNKS, relay_other)
+
+    def work(q):
+        for s in range(2):
+            loop(1, n, lambda k: incoming(s, q, k).wait_recv())
+            own_incoming(s, q).wait()
+        loop(
+            q * group,
+            (q + 1) * group,
+            functools.partial(
+                fold_row, True, scale, count, table, table_t, lesser_buf, other_buf, folded, volts
+            ),
+        )
+        loop(1, n, lambda k: outgoing(q, k).start())
+        own_outgoing(q).start()
+
+    loop(0, CHUNKS, work)
+    keeping = pltpu.make_async_copy(lesser_buf, kept, keep.at[0])
+    keeping.start()
+
+    def finish(q):
+        for s in range(2):
+            swap(s, q).wait_send()
+            loop(1, n, lambda k: incoming(s, q, k).wait_send())
+        loop(1, n, lambda k: outgoing(q, k).wait())
+        own_outgoing(q).wait()
+
+    loop(0, CHUNKS, finish)
+    keeping.wait()
+
+
+def dress_kernel(
+    n, count, scale, kept, screen, table, table_t, out,
+    lesser_buf, other_buf, folded, in_send, in_recv, out_send, out_recv, own_in, own_out, keep,
+):
+    place = Place(n)
+    me, plane, half = place.me, place.plane, place.half
+    rows = folded.shape[1]
+    each = count // n
+    group = rows // CHUNKS
+
+    def incoming(q, k):
+        peer = lax.rem(place.member + k, n)
+        return pltpu.make_async_remote_copy(
+            src_ref=screen.at[:, pl.ds((q * n + peer) * group, group)],
+            dst_ref=other_buf.at[:, pl.ds(q * group, group), pl.ds(place.member * each, each)],
+            send_sem=in_send.at[q, k],
+            recv_sem=in_recv.at[q, k],
+            device_id=place.of_member(peer),
+            device_id_type=MESH,
+        )
+
+    def own_incoming(q):
+        return pltpu.make_async_copy(
+            screen.at[:, pl.ds((q * n + place.member) * group, group)],
+            other_buf.at[:, pl.ds(q * group, group), pl.ds(place.member * each, each)],
+            own_in.at[q],
+        )
+
+    def outgoing(q, k, sender):
         peer = lax.rem(me + k, n)
         return pltpu.make_async_remote_copy(
             src_ref=folded.at[:, pl.ds(q * group, group), pl.ds(peer * each, each)],
-            dst_ref=out.at[:, pl.ds(me * rows + q * group, group)],
+            dst_ref=out.at[:, pl.ds((q * n + place.member) * group, group)],
             send_sem=out_send.at[q, k],
-            recv_sem=out_recv.at[q, k],
-            device_id={"ea": peer},
+            recv_sem=out_recv.at[q, sender],
+            device_id={"bias": half, "ea": peer},
             device_id_type=MESH,
         )
 
-    def own_incoming(s):
-        source, target = streams[s]
+    def own_outgoing(q):
         return pltpu.make_async_copy(
-            source.at[:, pl.ds(me * rows, rows)],
-            target.at[:, :, pl.ds(me * each, each)],
-            own_in.at[s],
-        )
-
-    def send_chunk(s, q):
-        def send_one(k, inner):
-            incoming(s, q, k).start()
-            return inner
-
-        lax.fori_loop(1, n, send_one, 0)
-
-    if first:
-        raw = (
-            pltpu.make_async_copy(lesser, lesser_raw, own_in.at[0]),
-            pltpu.make_async_copy(other, other_raw, own_in.at[1]),
-        )
-        for copy in raw:
-            copy.start()
-        greet(n)
-        raw[0].wait()
-        mine = pl.ds(pl.multiple_of(me * each, each), each)
-
-        def regroup(k, carry):
-            peer = lax.rem(me + k, n)
-            block = pl.ds(pl.multiple_of(peer * rows, rows), rows)
-            for c in range(2):
-                lesser_rows[c, block] = jnp.swapaxes(lesser_raw[:, c, block, :], 0, 1)
-            return carry
-
-        def regroup_and_send(k, carry):
-            regroup(k, carry)
-
-            def send_one(q, inner):
-                incoming(0, q, k).start()
-                return inner
-
-            return lax.fori_loop(0, CHUNKS, send_one, carry)
-
-        lax.fori_loop(1, n, regroup_and_send, 0)
-        regroup(0, 0)
-        raw[1].wait()
-        for low in range(0, rows * n, LANES):
-            for c in range(2):
-                turned = jnp.stack(
-                    [other_raw[e, c, :, low : low + LANES].T for e in range(each)], axis=0
-                )
-                other_rows[c, low : low + LANES] = jnp.swapaxes(turned, 0, 1)
-        lax.fori_loop(0, CHUNKS, lambda q, carry: (send_chunk(1, q), carry)[1], 0)
-        for source, target in streams:
-            for c in range(2):
-                target[c, :, mine, :] = source[c, pl.ds(me * rows, rows)]
-    else:
-        pltpu.make_async_copy(kept, lesser_buf, keep).start()
-        own_incoming(0).start()
-        greet(n)
-        lax.fori_loop(0, CHUNKS, lambda q, carry: (send_chunk(0, q), carry)[1], 0)
-        own_incoming(0).wait()
-        pltpu.make_async_copy(kept, lesser_buf, keep).wait()
-
-    length = 2 * count
-
-    def fold(row, carry):
-        left = jnp.concatenate([lesser_buf[0, row], lesser_buf[1, row]], axis=0)
-        imag = other_buf[1, row]
-        right = jnp.concatenate([other_buf[0, row], -imag if first else imag], axis=0)
-        left_spec = jnp.dot(table[...], left, preferred_element_type=jnp.float32)
-        right_spec = jnp.dot(table[...], right, preferred_element_type=jnp.float32)
-        left_real, left_imag = left_spec[:length], left_spec[length:]
-        right_real, right_imag = right_spec[:length], right_spec[length:]
-        if first:
-            real = left_real * right_real + left_imag * right_imag
-            imag = left_imag * right_real - left_real * right_imag
-        else:
-            real = left_real * right_real - left_imag * right_imag
-            imag = left_real * right_imag + left_imag * right_real
-        product = jnp.concatenate([real, imag], axis=0).astype(jnp.bfloat16)
-        result = jnp.dot(table_t[...], product, preferred_element_type=jnp.float32) * scale
-        result = result.astype(jnp.bfloat16)
-        if first:
-            result = jnp.dot(result, volts[...], preferred_element_type=jnp.float32)
-            result = result.astype(jnp.bfloat16)
-        folded[0, row] = result[:count]
-        folded[1, row] = result[count:]
-        return carry
-
-    def work(q, carry):
-        for s in range(len(streams)):
-            def wait_one(k, inner):
-                incoming(s, q, k).wait()
-                return inner
-            lax.fori_loop(1, n, wait_one, 0)
-        lax.fori_loop(q * group, (q + 1) * group, fold, 0)
-
-        def send_one(k, inner):
-            outgoing(q, k).start()
-            return inner
-
-        lax.fori_loop(1, n, send_one, 0)
-        return carry
-
-    lax.fori_loop(0, CHUNKS, work, 0)
-    own_result = pltpu.make_async_copy(
-        folded.at[:, :, pl.ds(me * each, each)], out.at[:, pl.ds(me * rows, rows)], own_out
-    )
-    own_result.start()
-    if first:
-        keeping = pltpu.make_async_copy(lesser_buf, kept, keep)
-        keeping.start()
-
-    def finish(q, carry):
-        def wait_one(k, inner):
-            outgoing(q, k).wait()
-            return inner
-        return lax.fori_loop(1, n, wait_one, carry)
-
-    lax.fori_loop(0, CHUNKS, finish, 0)
-    own_result.wait()
-    if first:
-        keeping.wait()
+            folded.at[:, pl.ds(q * group, group), pl.ds(me * each, each)],
+            out.at[:, pl.ds((q * n + place.member) * group, group)],
+            own_out.at[q],
+        )
+
+    at_home = plane == half
+    keeping = pltpu.make_async_copy(kept, lesser_buf, keep.at[0])
+    keeping.start()
+    loop(0, CHUNKS, lambda q: own_incoming(q).start())
+    greet(place)
+    loop(0, CHUNKS, lambda q: loop(1, n, lambda k: incoming(q, k).start()))
+    keeping.wait()
+
+    def work(q):
+        loop(1, n, lambda k: incoming(q, k).wait_recv())
+        own_incoming(q).wait()
+        loop(
+            q * group,
+            (q + 1) * group,
+            functools.partial(
+                fold_row, False, scale, count, table, table_t, lesser_buf, other_buf, folded, None
+            ),
+        )
+
+        @pl.when(at_home)
+        def _():
+            own_outgoing(q).start()
+
+        @pl.when(jnp.logical_not(at_home))
+        def _():
+            outgoing(q, 0, place.member).start()
+
+        loop(1, n, lambda k: outgoing(q, k, place.member).start())
+
+    loop(0, CHUNKS, work)
+
+    def finish(q):
+        loop(1, n, lambda k: incoming(q, k).wait_send())
+        loop(1, n, lambda k: outgoing(q, k, place.member).wait_send())
+
+        @pl.when(at_home)
+        def _():
+            own_outgoing(q).wait()
+
+        @pl.when(jnp.logical_not(at_home))
+        def _():
+            outgoing(q, 0, place.member).wait_send()
+
+        def wait_one(sender):
+            @pl.when(jnp.logical_not(jnp.logical_and(at_home, sender == place.member)))
+            def _():
+                outgoing(q, 0, sender).wait_recv()
+
+        loop(0, n, wait_one)
+
+    loop(0, CHUNKS, finish)
 
 
 def exchange(n, count, first, scale, operands):
@@ -332,28 +479,28 @@
     rows = orbitals // n
     hbm = pl.BlockSpec(memory_space=pl.ANY)
     vmem = pl.BlockSpec(memory_space=pltpu.VMEM)
-    streams = 2 if first else 1
     out_shape = [jax.ShapeDtypeStruct((2, orbitals, each, width), jnp.bfloat16)]
     if first:
         out_shape.append(jax.ShapeDtypeStruct((2, rows, count, width), jnp.bfloat16))
     buffer = pltpu.VMEM((2, rows, count, width), jnp.bfloat16)
     dma = pltpu.SemaphoreType.DMA
-    staging = []
+    lead = (2, CHUNKS) if first else (CHUNKS,)
+    scratch = [
+        buffer, buffer, buffer,
+        dma(lead + (n,)), dma(lead + (n,)), dma((CHUNKS, n)), dma((CHUNKS, n)),
+        dma(lead), dma((CHUNKS,)), dma((2,)),
+    ]
     if first:
-        staging = [pltpu.VMEM((each, 2, orbitals, width), jnp.bfloat16)] * 2
-        staging += [pltpu.VMEM((2, orbitals, each, width), jnp.bfloat16)] * 2
+        scratch += [dma((2, CHUNKS))] * 2
+        scratch += [pltpu.VMEM((each, 2, orbitals, width), jnp.bfloat16)] * 2
+        scratch += [pltpu.VMEM((3, 2, orbitals // 2, each, width), jnp.bfloat16)] * 2
     return pl.pallas_call(
-        functools.partial(exchange_kernel, n, count, first, scale),
+        functools.partial(polarize_kernel if first else dress_kernel, n, count, scale),
         name="polarize" if first else "dress",
         out_shape=out_shape,
         in_specs=[hbm, hbm] + [vmem] * (len(operands) - 2),
         out_specs=[hbm] * len(out_shape),
-        scratch_shapes=[
-            buffer, buffer, buffer,
-            dma((streams, CHUNKS, n)), dma((streams, CHUNKS, n)),
-            dma((CHUNKS, n)), dma((CHUNKS, n)),
-            dma((streams,)), dma, dma,
-        ] + staging,
+        scratch_shapes=scratch,
         compiler_params=pltpu.CompilerParams(
             collective_id=0 if first else 1, has_side_effects=True, vmem_limit_bytes=VMEM_BYTES
         ),
@@ -408,10 +555,10 @@
     )(matrices, *others)
 
 
-def per_device(n, g_lesser, g_greater, g_free, coulomb):
+def per_device(n, biases, g_lesser, g_greater, g_free, coulomb):
     each, _, orbitals, _ = g_lesser.shape
     count = n * each
-    if each % 16 or orbitals % (n * 16) or orbitals % LANES:
+    if biases != 2 or n % 2 or each % 16 or orbitals % (n * 16) or LANES % (n // 2 * orbitals // n // CHUNKS):
         return plain(g_lesser, g_greater, g_free, coulomb)
     scale = 1.0 / (2 * count * count)
     full = transform_table(count)
@@ -428,7 +575,7 @@
 
 def solution(mesh):
     return jax.shard_map(
-        functools.partial(per_device, mesh.shape["ea"]),
+        functools.partial(per_device, mesh.shape["ea"], mesh.shape["bias"]),
         mesh=mesh,
         in_specs=(
             P(("bias", "ea"), None, None, None),

time: 509 us -> 419 us (0.82)
  Pallas kernels: 491 us -> 400 us
    pallas_call x2, Pallas kernels: 469 us -> 379 us  [exchange(): pl.pallas_call(functools.partial(polarize_kernel if first else dress_kern...]
where the time goes in v1:
time: 419 us; the launch traced here: 418 us
  Pallas kernels  400 us (95%)
  local copies, waits for them, and re-layouts  17.9 us (4%)
    pallas_call x2, Pallas kernels, exchange(): pl.pallas_call(functools.partial(polarize_kernel if first else dress_kern...  379 us
    pallas_call x2, Pallas kernels, per_energy(): pl.pallas_call(kernel, name=name, grid=(each // 2,), out_shape=jax.ShapeD...  21.5 us
    pallas_call x2, local copies, waits for them, and re-layouts, exchange(): pl.pallas_call(functools.partial(polarize_kernel if first else dress_kern...  11.3 us

profile of v1, /device:TPU:15, one launch (start us, length us, event | category | flops | bytes accessed | tf_op | source)
XLA Modules:
  0.0 417.9 jit_solution(5190459999528439792)
XLA Ops:
  0.0 236.6 %polarize.1 = (bf16[2,256,16,256]{3,2,1,0:T(8,128)(2,1)}, bf16[2,16,256,256]{3,2,1,0:T(8,128)(2,1)}) custom-call(bf16[16,2,256,256]{3,2,1,0:T(8,128)(2,1)} %lesser.1, bf16[16,2,256,256]{3,2,1,0:T(8,128)(2,1)} %other.1, bf16[1024,512]{1,0:T(8,128)(2,1)} %constant.9.table, bf16[512,1024]{1,0:T(8,128)(2,1)} %constant.10.table_t, bf16[256,256]{1,0:T(8,128)(2,1)} %volts.3), custom_call_target="tpu_custom_call" | custom-call | tf_op jit(solution)/shard_map/polarize/pallas_call | solution.py:497
  236.6 5.7 %copy.15 = bf16[2,256,16,256]{3,1,0,2:T(8,128)(2,1)} copy(bf16[2,256,16,256]{3,2,1,0:T(8,128)(2,1)} %get-tuple-element.8) | data formatting | bytes 8388608 | tf_op jit(solution)/shard_map/polarize/pallas_call | solution.py:497
  242.3 10.2 %screen.1 = bf16[16,2,256,256]{3,2,1,0:T(8,128)(2,1)} custom-call(bf16[16,2,256,256]{3,2,1,0:T(8,128)(2,1)} %bitcast.10, bf16[256,256]{1,0:T(8,128)(2,1)} %volts.3), custom_call_target="tpu_custom_call" | custom-call | flops 3221225472 | bytes 8388608 | tf_op jit(solution)/shard_map/screen/pallas_call | solution.py:543
  252.4 6.6 %copy.14 = bf16[16,2,256,256]{3,0,2,1:T(8,128)(2,1)} copy(bf16[16,2,256,256]{3,2,1,0:T(8,128)(2,1)} %screen.1) | data formatting | bytes 8388608 | tf_op jit(solution)/shard_map/screen/pallas_call | solution.py:543
  259.0 141.9 %dress.1 = bf16[2,256,16,256]{3,2,1,0:T(8,128)(2,1)} custom-call(bf16[2,16,256,256]{3,2,1,0:T(8,128)(2,1)} %get-tuple-element.7.kept, bf16[2,256,16,256]{3,2,1,0:T(8,128)(2,1)} %bitcast.9, bf16[1024,512]{1,0:T(8,128)(2,1)} %constant.9.table, bf16[512,1024]{1,0:T(8,128)(2,1)} %constant.10.table_t), custom_call_target="tpu_custom_call" | custom-call | tf_op jit(solution)/shard_map/dress/pallas_call | solution.py:497
  400.9 5.6 %copy.13 = bf16[2,256,16,256]{3,1,0,2:T(8,128)(2,1)} copy(bf16[2,256,16,256]{3,2,1,0:T(8,128)(2,1)} %dress.1) | data formatting | bytes 8388608 | tf_op jit(solution)/shard_map/dress/pallas_call | solution.py:497
  406.5 11.3 %dyson.1 = bf16[16,2,256,256]{3,2,1,0:T(8,128)(2,1)} custom-call(bf16[16,2,256,256]{3,2,1,0:T(8,128)(2,1)} %bitcast.11, bf16[16,2,256,256]{3,2,1,0:T(8,128)(2,1)} %free.1), custom_call_target="tpu_custom_call" | custom-call | flops 4294967296 | bytes 8388608 | tf_op jit(solution)/shard_map/dyson/pallas_call | solution.py:543

commit v2 on v1

--- a/solution.py
+++ b/solution.py
@@ -134,7 +134,8 @@
 
 
 MESH = pl.DeviceIdType.MESH
-CHUNKS = 4
+CHUNKS = 8
+AHEAD = 2
 LANES = 128
 VMEM_BYTES = 60 * 1024 * 1024
 
@@ -315,11 +316,8 @@
                     lesser_raw[:, c, block, :], 0, 1
                 )
         swap(0, q).start()
-        spread(0, q, plane)
-
-    loop(0, CHUNKS, regroup)
-    raw[1].wait()
-    for low in range(0, rows * n, LANES):
+
+    def turn(low):
         for c in range(2):
             turned = jnp.stack(
                 [other_raw[e, c, :, low : low + LANES].T for e in range(each)], axis=0
@@ -330,22 +328,48 @@
                 slot = jnp.where(plane == piece % 2, piece % 2, 2)
                 start = piece // 2 * wide
                 other_rows[slot, c, start : start + wide] = turned[at : at + wide]
-    loop(0, CHUNKS, lambda q: swap(1, q).start())
-
-    def relay(q):
-        swap(0, q).wait_recv()
-        spread(0, q, 1 - plane)
-
-    loop(0, CHUNKS, relay)
-
-    def relay_other(q):
+
+    def relay(s, q):
+        swap(s, q).wait_recv()
+        spread(s, q, 1 - plane)
+
+    def advance(q):
+        for s in range(2):
+            spread(s, q, plane)
+            relay(s, q)
+
+    def own_first(q):
+        regroup(q)
+        spread(0, q, plane)
+
+    def both(q):
+        regroup(q)
+        swap(1, q).start()
+
+    per = LANES // (2 * wide)
+    loop(0, AHEAD, own_first)
+    raw[1].wait()
+    turn(0)
+    loop(0, AHEAD, lambda q: swap(1, q).start())
+    spread(1, 0, plane)
+    loop(0, AHEAD, lambda q: relay(0, q))
+    loop(AHEAD, per, both)
+    for low in range(LANES, rows * n, LANES):
+        turn(low)
+        loop(low // LANES * per, (low // LANES + 1) * per, both)
+    relay(1, 0)
+
+    def rest(q):
         spread(1, q, plane)
-        swap(1, q).wait_recv()
-        spread(1, q, 1 - plane)
-
-    loop(0, CHUNKS, relay_other)
+        relay(1, q)
+
+    loop(1, AHEAD, rest)
 
     def work(q):
+        @pl.when(q + AHEAD < CHUNKS)
+        def _():
+            advance(q + AHEAD)
+
         for s in range(2):
             loop(1, n, lambda k: incoming(s, q, k).wait_recv())
             own_incoming(s, q).wait()
@@ -439,6 +463,16 @@
             ),
         )
 
+        def far(j):
+            peer = (1 - half) * place.side + lax.rem(place.seat + j, place.side)
+            outgoing(q, lax.rem(peer - me + n, n), place.member).start()
+
+        def near(j):
+            peer = half * place.side + lax.rem(place.seat + j, place.side)
+            outgoing(q, lax.rem(peer - me + n, n), place.member).start()
+
+        loop(0, place.side, far)
+
         @pl.when(at_home)
         def _():
             own_outgoing(q).start()
@@ -447,7 +481,7 @@
         def _():
             outgoing(q, 0, place.member).start()
 
-        loop(1, n, lambda k: outgoing(q, k, place.member).start())
+        loop(1, place.side, near)
 
     loop(0, CHUNKS, work)
 

time: 419 us -> 392 us (0.936)
  Pallas kernels: 400 us -> 372 us
    pallas_call x2, Pallas kernels: 379 us -> 351 us  [exchange(): pl.pallas_call(functools.partial(polarize_kernel if first else dress_kern...]
where the time goes in v2:
time: 392 us; the launch traced here: 390 us
  Pallas kernels  372 us (95%)
  local copies, waits for them, and re-layouts  17.9 us (5%)
    pallas_call x2, Pallas kernels, exchange(): pl.pallas_call(functools.partial(polarize_kernel if first else dress_kern...  351 us
    pallas_call x2, Pallas kernels, per_energy(): pl.pallas_call(kernel, name=name, grid=(each // 2,), out_shape=jax.ShapeD...  21.5 us
    pallas_call x2, local copies, waits for them, and re-layouts, exchange(): pl.pallas_call(functools.partial(polarize_kernel if first else dress_kern...  11.3 us

profile of v2, /device:TPU:15, one launch (start us, length us, event | category | flops | bytes accessed | tf_op | source)
XLA Modules:
  0.0 390.2 jit_solution(17136526422477613690)
XLA Ops:
  0.0 213.1 %polarize.1 = (bf16[2,256,16,256]{3,2,1,0:T(8,128)(2,1)}, bf16[2,16,256,256]{3,2,1,0:T(8,128)(2,1)}) custom-call(bf16[16,2,256,256]{3,2,1,0:T(8,128)(2,1)} %lesser.1, bf16[16,2,256,256]{3,2,1,0:T(8,128)(2,1)} %other.1, bf16[1024,512]{1,0:T(8,128)(2,1)} %constant.9.table, bf16[512,1024]{1,0:T(8,128)(2,1)} %constant.10.table_t, bf16[256,256]{1,0:T(8,128)(2,1)} %volts.3), custom_call_target="tpu_custom_call" | custom-call | tf_op jit(solution)/shard_map/polarize/pallas_call | solution.py:531
  213.1 5.7 %copy.15 = bf16[2,256,16,256]{3,1,0,2:T(8,128)(2,1)} copy(bf16[2,256,16,256]{3,2,1,0:T(8,128)(2,1)} %get-tuple-element.8) | data formatting | bytes 8388608 | tf_op jit(solution)/shard_map/polarize/pallas_call | solution.py:531
  218.8 10.2 %screen.1 = bf16[16,2,256,256]{3,2,1,0:T(8,128)(2,1)} custom-call(bf16[16,2,256,256]{3,2,1,0:T(8,128)(2,1)} %bitcast.10, bf16[256,256]{1,0:T(8,128)(2,1)} %volts.3), custom_call_target="tpu_custom_call" | custom-call | flops 3221225472 | bytes 8388608 | tf_op jit(solution)/shard_map/screen/pallas_call | solution.py:577
  228.9 6.6 %copy.14 = bf16[16,2,256,256]{3,0,2,1:T(8,128)(2,1)} copy(bf16[16,2,256,256]{3,2,1,0:T(8,128)(2,1)} %screen.1) | data formatting | bytes 8388608 | tf_op jit(solution)/shard_map/screen/pallas_call | solution.py:577
  235.5 137.8 %dress.1 = bf16[2,256,16,256]{3,2,1,0:T(8,128)(2,1)} custom-call(bf16[2,16,256,256]{3,2,1,0:T(8,128)(2,1)} %get-tuple-element.7.kept, bf16[2,256,16,256]{3,2,1,0:T(8,128)(2,1)} %bitcast.9, bf16[1024,512]{1,0:T(8,128)(2,1)} %constant.9.table, bf16[512,1024]{1,0:T(8,128)(2,1)} %constant.10.table_t), custom_call_target="tpu_custom_call" | custom-call | tf_op jit(solution)/shard_map/dress/pallas_call | solution.py:531
  373.3 5.6 %copy.13 = bf16[2,256,16,256]{3,1,0,2:T(8,128)(2,1)} copy(bf16[2,256,16,256]{3,2,1,0:T(8,128)(2,1)} %dress.1) | data formatting | bytes 8388608 | tf_op jit(solution)/shard_map/dress/pallas_call | solution.py:531
  378.9 11.3 %dyson.1 = bf16[16,2,256,256]{3,2,1,0:T(8,128)(2,1)} custom-call(bf16[16,2,256,256]{3,2,1,0:T(8,128)(2,1)} %bitcast.11, bf16[16,2,256,256]{3,2,1,0:T(8,128)(2,1)} %free.1), custom_call_target="tpu_custom_call" | custom-call | flops 4294967296 | bytes 8388608 | tf_op jit(solution)/shard_map/dyson/pallas_call | solution.py:577

commit v3 on v2

--- a/solution.py
+++ b/solution.py
@@ -136,6 +136,7 @@
 MESH = pl.DeviceIdType.MESH
 CHUNKS = 8
 AHEAD = 2
+BEHIND = 2
 LANES = 128
 VMEM_BYTES = 60 * 1024 * 1024
 
@@ -217,19 +218,23 @@
     folded[1, row] = result[count:]
 
 
-def polarize_kernel(
-    n, count, scale, lesser, other, table, table_t, volts, out, kept,
-    lesser_buf, other_buf, folded, in_send, in_recv, out_send, out_recv, own_in, own_out, keep,
-    swap_send, swap_recv, lesser_raw, other_raw, lesser_rows, other_rows,
+def gw_kernel(
+    n, count, scale, lesser, other, table, table_t, volts, out,
+    lesser_buf, other_buf, folded, lesser_raw, other_raw, lesser_rows, other_rows,
+    mixed, screen, sigma,
+    in_send, in_recv, own_in, swap_send, swap_recv, p_send, p_recv, p_own,
+    w_send, w_recv, w_own, s_send, s_recv, s_own, keep,
 ):
     place = Place(n)
     me, plane, half, side = place.me, place.plane, place.half, place.side
+    member = place.member
     rows = folded.shape[1]
     each = count // n
     group = rows // CHUNKS
     wide = side * group
     stages = (lesser_rows, other_rows)
     targets = (lesser_buf, other_buf)
+    at_home = plane == half
 
     def swap(s, q):
         span = pl.ds(q * wide, wide)
@@ -280,22 +285,61 @@
 
         loop(0, side, send_one)
 
-    def outgoing(q, k):
-        peer = lax.rem(place.member + k, n)
+    def mine(q):
+        return pl.ds((q * n + member) * group, group)
+
+    def polar(q, k):
+        peer = lax.rem(member + k, n)
         return pltpu.make_async_remote_copy(
             src_ref=folded.at[:, pl.ds(q * group, group), pl.ds(peer * each, each)],
-            dst_ref=out.at[:, pl.ds((q * n + place.member) * group, group)],
-            send_sem=out_send.at[q, k],
-            recv_sem=out_recv.at[q, k],
+            dst_ref=mixed.at[:, mine(q)],
+            send_sem=p_send.at[q, k],
+            recv_sem=p_recv.at[q, k],
             device_id=place.of_member(peer),
             device_id_type=MESH,
         )
 
-    def own_outgoing(q):
+    def own_polar(q):
         return pltpu.make_async_copy(
-            folded.at[:, pl.ds(q * group, group), pl.ds(place.member * each, each)],
-            out.at[:, pl.ds((q * n + place.member) * group, group)],
-            own_out.at[q],
+            folded.at[:, pl.ds(q * group, group), pl.ds(member * each, each)],
+            mixed.at[:, mine(q)],
+            p_own.at[q],
+        )
+
+    def screened(q, k):
+        peer = lax.rem(member + k, n)
+        return pltpu.make_async_remote_copy(
+            src_ref=screen.at[:, pl.ds((q * n + peer) * group, group)],
+            dst_ref=other_buf.at[:, pl.ds(q * group, group), pl.ds(member * each, each)],
+            send_sem=w_send.at[q, k],
+            recv_sem=w_recv.at[q, k],
+            device_id=place.of_member(peer),
+            device_id_type=MESH,
+        )
+
+    def own_screened(q):
+        return pltpu.make_async_copy(
+            screen.at[:, mine(q)],
+            other_buf.at[:, pl.ds(q * group, group), pl.ds(member * each, each)],
+            w_own.at[q],
+        )
+
+    def dressed(q, k, sender):
+        peer = lax.rem(me + k, n)
+        return pltpu.make_async_remote_copy(
+            src_ref=folded.at[:, pl.ds(q * group, group), pl.ds(peer * each, each)],
+            dst_ref=sigma.at[:, mine(q)],
+            send_sem=s_send.at[q, k],
+            recv_sem=s_recv.at[q, sender],
+            device_id={"bias": half, "ea": peer},
+            device_id_type=MESH,
+        )
+
+    def own_dressed(q):
+        return pltpu.make_async_copy(
+            folded.at[:, pl.ds(q * group, group), pl.ds(me * each, each)],
+            sigma.at[:, mine(q)],
+            s_own.at[q],
         )
 
     raw = (
@@ -365,6 +409,15 @@
 
     loop(1, AHEAD, rest)
 
+    def chunk_rows(q):
+        return pl.ds(pl.multiple_of(q * 2 * wide, 2 * wide), 2 * wide)
+
+    def absorb(q):
+        loop(1, n, lambda k: polar(q, k).wait_recv())
+        own_polar(q).wait()
+        for c in range(2):
+            lesser_raw[:, c, chunk_rows(q), :] = jnp.swapaxes(mixed[c, chunk_rows(q)], 0, 1)
+
     def work(q):
         @pl.when(q + AHEAD < CHUNKS)
         def _():
@@ -380,81 +433,56 @@
                 fold_row, True, scale, count, table, table_t, lesser_buf, other_buf, folded, volts
             ),
         )
-        loop(1, n, lambda k: outgoing(q, k).start())
-        own_outgoing(q).start()
+        loop(1, n, lambda k: polar(q, k).start())
+        own_polar(q).start()
+
+        @pl.when(q >= BEHIND)
+        def _():
+            absorb(q - BEHIND)
 
     loop(0, CHUNKS, work)
-    keeping = pltpu.make_async_copy(lesser_buf, kept, keep.at[0])
-    keeping.start()
-
-    def finish(q):
+    loop(CHUNKS - BEHIND, CHUNKS, absorb)
+    bare = volts[...]
+    width = bare.shape[0]
+
+    def screen_one(e):
+        pair = lesser_raw[e].reshape(2 * width, width)
+        by_real = dot(pair, lesser_raw[e, 0])
+        by_imag = dot(pair, lesser_raw[e, 1])
+        square_real = by_real[:width] - by_imag[width:]
+        square_imag = by_imag[:width] + by_real[width:]
+        inner = jnp.concatenate(
+            [
+                (lesser_raw[e, 0].astype(jnp.float32) + square_real).astype(jnp.bfloat16),
+                (lesser_raw[e, 1].astype(jnp.float32) + square_imag).astype(jnp.bfloat16),
+            ],
+            axis=1,
+        )
+        result = dot(bare, inner)
+        lesser_raw[e, 0] = (bare.astype(jnp.float32) + result[:, :width]).astype(jnp.bfloat16)
+        lesser_raw[e, 1] = result[:, width:].astype(jnp.bfloat16)
+
+    loop(0, each, screen_one)
+
+    def send_screen(q):
+        for c in range(2):
+            screen[c, chunk_rows(q)] = jnp.swapaxes(lesser_raw[:, c, chunk_rows(q), :], 0, 1)
+        loop(1, n, lambda k: screened(q, k).start())
+        own_screened(q).start()
+
+    loop(0, CHUNKS, send_screen)
+
+    def settle(q):
         for s in range(2):
             swap(s, q).wait_send()
             loop(1, n, lambda k: incoming(s, q, k).wait_send())
-        loop(1, n, lambda k: outgoing(q, k).wait())
-        own_outgoing(q).wait()
-
-    loop(0, CHUNKS, finish)
-    keeping.wait()
-
-
-def dress_kernel(
-    n, count, scale, kept, screen, table, table_t, out,
-    lesser_buf, other_buf, folded, in_send, in_recv, out_send, out_recv, own_in, own_out, keep,
-):
-    place = Place(n)
-    me, plane, half = place.me, place.plane, place.half
-    rows = folded.shape[1]
-    each = count // n
-    group = rows // CHUNKS
-
-    def incoming(q, k):
-        peer = lax.rem(place.member + k, n)
-        return pltpu.make_async_remote_copy(
-            src_ref=screen.at[:, pl.ds((q * n + peer) * group, group)],
-            dst_ref=other_buf.at[:, pl.ds(q * group, group), pl.ds(place.member * each, each)],
-            send_sem=in_send.at[q, k],
-            recv_sem=in_recv.at[q, k],
-            device_id=place.of_member(peer),
-            device_id_type=MESH,
-        )
-
-    def own_incoming(q):
-        return pltpu.make_async_copy(
-            screen.at[:, pl.ds((q * n + place.member) * group, group)],
-            other_buf.at[:, pl.ds(q * group, group), pl.ds(place.member * each, each)],
-            own_in.at[q],
-        )
-
-    def outgoing(q, k, sender):
-        peer = lax.rem(me + k, n)
-        return pltpu.make_async_remote_copy(
-            src_ref=folded.at[:, pl.ds(q * group, group), pl.ds(peer * each, each)],
-            dst_ref=out.at[:, pl.ds((q * n + place.member) * group, group)],
-            send_sem=out_send.at[q, k],
-            recv_sem=out_recv.at[q, sender],
-            device_id={"bias": half, "ea": peer},
-            device_id_type=MESH,
-        )
-
-    def own_outgoing(q):
-        return pltpu.make_async_copy(
-            folded.at[:, pl.ds(q * group, group), pl.ds(me * each, each)],
-            out.at[:, pl.ds((q * n + place.member) * group, group)],
-            own_out.at[q],
-        )
-
-    at_home = plane == half
-    keeping = pltpu.make_async_copy(kept, lesser_buf, keep.at[0])
-    keeping.start()
-    loop(0, CHUNKS, lambda q: own_incoming(q).start())
-    greet(place)
-    loop(0, CHUNKS, lambda q: loop(1, n, lambda k: incoming(q, k).start()))
-    keeping.wait()
-
-    def work(q):
-        loop(1, n, lambda k: incoming(q, k).wait_recv())
-        own_incoming(q).wait()
+        loop(1, n, lambda k: polar(q, k).wait_send())
+
+    loop(0, CHUNKS, settle)
+
+    def dress(q):
+        loop(1, n, lambda k: screened(q, k).wait_recv())
+        own_screened(q).wait()
         loop(
             q * group,
             (q + 1) * group,
@@ -463,98 +491,91 @@
             ),
         )
 
-        def far(j):
-            peer = (1 - half) * place.side + lax.rem(place.seat + j, place.side)
-            outgoing(q, lax.rem(peer - me + n, n), place.member).start()
-
-        def near(j):
-            peer = half * place.side + lax.rem(place.seat + j, place.side)
-            outgoing(q, lax.rem(peer - me + n, n), place.member).start()
-
-        loop(0, place.side, far)
+        def send_to(target_half):
+            def send_one(j):
+                peer = target_half * side + lax.rem(place.seat + j, side)
+                dressed(q, lax.rem(peer - me + n, n), member).start()
+
+            return send_one
+
+        loop(0, side, send_to(1 - half))
 
         @pl.when(at_home)
         def _():
-            own_outgoing(q).start()
+            own_dressed(q).start()
 
         @pl.when(jnp.logical_not(at_home))
         def _():
-            outgoing(q, 0, place.member).start()
-
-        loop(1, place.side, near)
-
-    loop(0, CHUNKS, work)
-
-    def finish(q):
-        loop(1, n, lambda k: incoming(q, k).wait_send())
-        loop(1, n, lambda k: outgoing(q, k, place.member).wait_send())
-
+            dressed(q, 0, member).start()
+
+        loop(1, side, send_to(half))
+
+    loop(0, CHUNKS, dress)
+
+    def collect(q):
         @pl.when(at_home)
         def _():
-            own_outgoing(q).wait()
+            own_dressed(q).wait()
+
+        def wait_one(sender):
+            @pl.when(jnp.logical_not(jnp.logical_and(at_home, sender == member)))
+            def _():
+                dressed(q, 0, sender).wait_recv()
+
+        loop(0, n, wait_one)
+        for c in range(2):
+            lesser_raw[:, c, chunk_rows(q), :] = jnp.swapaxes(sigma[c, chunk_rows(q)], 0, 1)
+
+    loop(0, CHUNKS, collect)
+    result = pltpu.make_async_copy(lesser_raw, out, keep.at[0])
+    result.start()
+
+    def finish(q):
+        loop(1, n, lambda k: screened(q, k).wait_send())
+        loop(1, n, lambda k: dressed(q, k, member).wait_send())
 
         @pl.when(jnp.logical_not(at_home))
         def _():
-            outgoing(q, 0, place.member).wait_send()
-
-        def wait_one(sender):
-            @pl.when(jnp.logical_not(jnp.logical_and(at_home, sender == place.member)))
-            def _():
-                outgoing(q, 0, sender).wait_recv()
-
-        loop(0, n, wait_one)
+            dressed(q, 0, member).wait_send()
 
     loop(0, CHUNKS, finish)
-
-
-def exchange(n, count, first, scale, operands):
-    orbitals, width = operands[1].shape[-3 if not first else -2], operands[1].shape[-1]
-    each = count // n
+    result.wait()
+
+
+def iterate(n, count, scale, g_lesser, g_greater, table, table_t, coulomb):
+    each, _, orbitals, width = g_lesser.shape
     rows = orbitals // n
     hbm = pl.BlockSpec(memory_space=pl.ANY)
     vmem = pl.BlockSpec(memory_space=pltpu.VMEM)
-    out_shape = [jax.ShapeDtypeStruct((2, orbitals, each, width), jnp.bfloat16)]
-    if first:
-        out_shape.append(jax.ShapeDtypeStruct((2, rows, count, width), jnp.bfloat16))
-    buffer = pltpu.VMEM((2, rows, count, width), jnp.bfloat16)
+    by_row = pltpu.VMEM((2, rows, count, width), jnp.bfloat16)
+    by_energy = pltpu.VMEM((each, 2, orbitals, width), jnp.bfloat16)
+    stage = pltpu.VMEM((3, 2, orbitals // 2, each, width), jnp.bfloat16)
+    landing = pltpu.VMEM((2, orbitals, each, width), jnp.bfloat16)
     dma = pltpu.SemaphoreType.DMA
-    lead = (2, CHUNKS) if first else (CHUNKS,)
-    scratch = [
-        buffer, buffer, buffer,
-        dma(lead + (n,)), dma(lead + (n,)), dma((CHUNKS, n)), dma((CHUNKS, n)),
-        dma(lead), dma((CHUNKS,)), dma((2,)),
-    ]
-    if first:
-        scratch += [dma((2, CHUNKS))] * 2
-        scratch += [pltpu.VMEM((each, 2, orbitals, width), jnp.bfloat16)] * 2
-        scratch += [pltpu.VMEM((3, 2, orbitals // 2, each, width), jnp.bfloat16)] * 2
+    pairs = dma((CHUNKS, n))
     return pl.pallas_call(
-        functools.partial(polarize_kernel if first else dress_kernel, n, count, scale),
-        name="polarize" if first else "dress",
-        out_shape=out_shape,
-        in_specs=[hbm, hbm] + [vmem] * (len(operands) - 2),
-        out_specs=[hbm] * len(out_shape),
-        scratch_shapes=scratch,
+        functools.partial(gw_kernel, n, count, scale),
+        name="iterate",
+        out_shape=jax.ShapeDtypeStruct(g_lesser.shape, jnp.bfloat16),
+        in_specs=[hbm, hbm, vmem, vmem, vmem],
+        out_specs=hbm,
+        scratch_shapes=[
+            by_row, by_row, by_row, by_energy, by_energy, stage, stage,
+            landing, landing, landing,
+            dma((2, CHUNKS, n)), dma((2, CHUNKS, n)), dma((2, CHUNKS)),
+            dma((2, CHUNKS)), dma((2, CHUNKS)),
+            pairs, pairs, dma((CHUNKS,)),
+            pairs, pairs, dma((CHUNKS,)),
+            pairs, pairs, dma((CHUNKS,)), dma((2,)),
+        ],
         compiler_params=pltpu.CompilerParams(
-            collective_id=0 if first else 1, has_side_effects=True, vmem_limit_bytes=VMEM_BYTES
+            collective_id=0, has_side_effects=True, vmem_limit_bytes=VMEM_BYTES
         ),
-    )(*operands)
+    )(g_lesser, g_greater, table, table_t, coulomb)
 
 
 def dot(left, right):
     return jnp.dot(left, right, preferred_element_type=jnp.float32)
-
-
-def screen_kernel(mixed, volts, out):
-    bare = volts[...]
-    for e in range(mixed.shape[0]):
-        real, imag = mixed[e, 0], mixed[e, 1]
-        square_real = dot(real, real) - dot(imag, imag)
-        square_imag = dot(real, imag) + dot(imag, real)
-        inner_real = (real.astype(jnp.float32) + square_real).astype(jnp.bfloat16)
-        inner_imag = (imag.astype(jnp.float32) + square_imag).astype(jnp.bfloat16)
-        out[e, 0] = (bare.astype(jnp.float32) + dot(bare, inner_real)).astype(jnp.bfloat16)
-        out[e, 1] = dot(bare, inner_imag).astype(jnp.bfloat16)
 
 
 def dyson_kernel(sigma, free, out):
@@ -598,12 +619,7 @@
     full = transform_table(count)
     table = jnp.asarray(full).astype(jnp.bfloat16)
     table_t = jnp.asarray(full.T).astype(jnp.bfloat16)
-    mixed, kept = exchange(n, count, True, scale, (g_lesser, g_greater, table, table_t, coulomb))
-    mixed = jnp.transpose(mixed, (2, 0, 1, 3))
-    screen = per_energy(screen_kernel, "screen", mixed, (coulomb,))
-    screen = jnp.transpose(screen, (1, 2, 0, 3))
-    (sigma,) = exchange(n, count, False, scale, (kept, screen, table, table_t))
-    sigma = jnp.transpose(sigma, (2, 0, 1, 3))
+    sigma = iterate(n, count, scale, g_lesser, g_greater, table, table_t, coulomb)
     return per_energy(dyson_kernel, "dyson", sigma, (g_free,))
 
 

time: 392 us -> 368 us (0.939); the launches traced: 390 us -> 362 us
  local copies, waits for them, and re-layouts: 17.9 us -> 0 us
  Pallas kernels: 372 us -> 362 us
    pallas_call x3 -> x0, local copies, waits for them, and re-layouts: 17.9 us -> none  [the longest x2 11.3 us: exchange(): pl.pallas_call(functools.partial(polarize_kernel if first else dress_kern...]
    pallas_call x2 -> x1, Pallas kernels: 21.5 us -> 11.3 us  [per_energy(): pl.pallas_call(kernel, name=name, grid=(each // 2,), out_shape=jax.ShapeD...]
    pallas_call x2 -> x1, Pallas kernels: 351 us -> 351 us  [iterate(): pl.pallas_call(functools.partial(gw_kernel, n, count, scale), name='itera...]
where the time goes in v3:
time: 368 us; the launch traced here: 362 us
  Pallas kernels  362 us (98%)
    pallas_call x1, Pallas kernels, iterate(): pl.pallas_call(functools.partial(gw_kernel, n, count, scale), name='itera...  351 us
    pallas_call x1, Pallas kernels, per_energy(): pl.pallas_call(kernel, name=name, grid=(each // 2,), out_shape=jax.ShapeD...  11.3 us

profile of v3, /device:TPU:15, one launch (start us, length us, event | category | flops | bytes accessed | tf_op | source)
XLA Modules:
  0.0 362.2 jit_solution(8427030188127629428)
XLA Ops:
  0.0 350.8 %iterate.1.sigma = bf16[16,2,256,256]{3,2,1,0:T(8,128)(2,1)} custom-call(bf16[16,2,256,256]{3,2,1,0:T(8,128)(2,1)} %lesser.1, bf16[16,2,256,256]{3,2,1,0:T(8,128)(2,1)} %other.1, bf16[1024,512]{1,0:T(8,128)(2,1)} %constant.9.table, bf16[512,1024]{1,0:T(8,128)(2,1)} %constant.10.table_t, bf16[256,256]{1,0:T(8,128)(2,1)} %volts.1), custom_call_target="tpu_custom_call" | custom-call | tf_op jit(solution)/shard_map/iterate/pallas_call | solution.py:556
  350.8 11.3 %dyson.1 = bf16[16,2,256,256]{3,2,1,0:T(8,128)(2,1)} custom-call(bf16[16,2,256,256]{3,2,1,0:T(8,128)(2,1)} %iterate.1.sigma, bf16[16,2,256,256]{3,2,1,0:T(8,128)(2,1)} %free.1), custom_call_target="tpu_custom_call" | custom-call | flops 4294967296 | bytes 8388608 | tf_op jit(solution)/shard_map/dyson/pallas_call | solution.py:598

commit v4 on v3

--- a/solution.py
+++ b/solution.py
@@ -134,9 +134,10 @@
 
 
 MESH = pl.DeviceIdType.MESH
-CHUNKS = 8
-AHEAD = 2
-BEHIND = 2
+CHUNKS = 16
+AHEAD = 6
+BEHIND = 4
+UNROLL = 4
 LANES = 128
 VMEM_BYTES = 60 * 1024 * 1024
 
@@ -222,8 +223,7 @@
     n, count, scale, lesser, other, table, table_t, volts, out,
     lesser_buf, other_buf, folded, lesser_raw, other_raw, lesser_rows, other_rows,
     mixed, screen, sigma,
-    in_send, in_recv, own_in, swap_send, swap_recv, p_send, p_recv, p_own,
-    w_send, w_recv, w_own, s_send, s_recv, s_own, keep,
+    in_send, in_recv, swap_send, swap_recv, p_send, p_recv, w_send, w_recv, s_send, s_recv, keep,
 ):
     place = Place(n)
     me, plane, half, side = place.me, place.plane, place.half, place.side
@@ -260,15 +260,15 @@
         return pltpu.make_async_remote_copy(
             src_ref=source,
             dst_ref=target,
-            send_sem=in_send.at[s, q, k],
-            recv_sem=in_recv.at[s, q, k],
+            send_sem=in_send.at[s, q],
+            recv_sem=in_recv.at[s, q],
             device_id={"ea": peer},
             device_id_type=MESH,
         )
 
     def own_incoming(s, q):
         source, target = ends(s, q, me)
-        return pltpu.make_async_copy(source, target, own_in.at[s, q])
+        return pltpu.make_async_copy(source, target, in_recv.at[s, q])
 
     def spread(s, q, bias):
         def send_one(j):
@@ -293,8 +293,8 @@
         return pltpu.make_async_remote_copy(
             src_ref=folded.at[:, pl.ds(q * group, group), pl.ds(peer * each, each)],
             dst_ref=mixed.at[:, mine(q)],
-            send_sem=p_send.at[q, k],
-            recv_sem=p_recv.at[q, k],
+            send_sem=p_send.at[q],
+            recv_sem=p_recv.at[q],
             device_id=place.of_member(peer),
             device_id_type=MESH,
         )
@@ -303,7 +303,7 @@
         return pltpu.make_async_copy(
             folded.at[:, pl.ds(q * group, group), pl.ds(member * each, each)],
             mixed.at[:, mine(q)],
-            p_own.at[q],
+            p_recv.at[q],
         )
 
     def screened(q, k):
@@ -311,8 +311,8 @@
         return pltpu.make_async_remote_copy(
             src_ref=screen.at[:, pl.ds((q * n + peer) * group, group)],
             dst_ref=other_buf.at[:, pl.ds(q * group, group), pl.ds(member * each, each)],
-            send_sem=w_send.at[q, k],
-            recv_sem=w_recv.at[q, k],
+            send_sem=w_send.at[q],
+            recv_sem=w_recv.at[q],
             device_id=place.of_member(peer),
             device_id_type=MESH,
         )
@@ -321,16 +321,16 @@
         return pltpu.make_async_copy(
             screen.at[:, mine(q)],
             other_buf.at[:, pl.ds(q * group, group), pl.ds(member * each, each)],
-            w_own.at[q],
-        )
-
-    def dressed(q, k, sender):
+            w_recv.at[q],
+        )
+
+    def dressed(q, k):
         peer = lax.rem(me + k, n)
         return pltpu.make_async_remote_copy(
             src_ref=folded.at[:, pl.ds(q * group, group), pl.ds(peer * each, each)],
             dst_ref=sigma.at[:, mine(q)],
-            send_sem=s_send.at[q, k],
-            recv_sem=s_recv.at[q, sender],
+            send_sem=s_send.at[q],
+            recv_sem=s_recv.at[q],
             device_id={"bias": half, "ea": peer},
             device_id_type=MESH,
         )
@@ -339,8 +339,17 @@
         return pltpu.make_async_copy(
             folded.at[:, pl.ds(q * group, group), pl.ds(me * each, each)],
             sigma.at[:, mine(q)],
-            s_own.at[q],
-        )
+            s_recv.at[q],
+        )
+
+    def await_all(ref, sem):
+        pltpu.make_async_copy(ref, ref, sem).wait()
+
+    def chunk(ref, q):
+        return ref.at[:, pl.ds(q * group, group)]
+
+    def sent(ref, q, pieces):
+        return ref.at[:, pl.ds(q * group, group), pl.ds(0, pieces * each)]
 
     raw = (
         pltpu.make_async_copy(lesser, lesser_raw, keep.at[0]),
@@ -351,27 +360,25 @@
     greet(place)
     raw[0].wait()
 
+    def chunk_rows(q):
+        return pl.ds(pl.multiple_of(q * 2 * wide, 2 * wide), 2 * wide)
+
     def regroup(q):
-        for h in range(2):
-            slot = jnp.where(plane == h, h, 2)
-            block = pl.ds(pl.multiple_of((2 * q + h) * wide, wide), wide)
-            for c in range(2):
-                lesser_rows[slot, c, pl.ds(pl.multiple_of(q * wide, wide), wide)] = jnp.swapaxes(
-                    lesser_raw[:, c, block, :], 0, 1
-                )
+        for c in range(2):
+            turned = jnp.swapaxes(lesser_raw[:, c, chunk_rows(q), :], 0, 1)
+            for h in range(2):
+                slot = jnp.where(plane == h, h, 2)
+                lesser_rows[slot, c, pl.ds(q * wide, wide)] = turned[h * wide : (h + 1) * wide]
         swap(0, q).start()
 
-    def turn(low):
-        for c in range(2):
-            turned = jnp.stack(
-                [other_raw[e, c, :, low : low + LANES].T for e in range(each)], axis=0
-            )
-            turned = jnp.swapaxes(turned, 0, 1)
-            for at in range(0, LANES, wide):
-                piece = (low + at) // wide
-                slot = jnp.where(plane == piece % 2, piece % 2, 2)
-                start = piece // 2 * wide
-                other_rows[slot, c, start : start + wide] = turned[at : at + wide]
+    def turn(low, c):
+        turned = jnp.stack([other_raw[e, c, :, low : low + LANES].T for e in range(each)], axis=0)
+        turned = jnp.swapaxes(turned, 0, 1)
+        for at in range(0, LANES, wide):
+            piece = (low + at) // wide
+            slot = jnp.where(plane == piece % 2, piece % 2, 2)
+            start = piece // 2 * wide
+            other_rows[slot, c, start : start + wide] = turned[at : at + wide]
 
     def relay(s, q):
         swap(s, q).wait_recv()
@@ -392,40 +399,48 @@
 
     per = LANES // (2 * wide)
     loop(0, AHEAD, own_first)
+    relay(0, 0)
     raw[1].wait()
-    turn(0)
+    turn(0, 0)
+    loop(1, AHEAD // 2 + 1, lambda q: relay(0, q))
+    turn(0, 1)
     loop(0, AHEAD, lambda q: swap(1, q).start())
     spread(1, 0, plane)
-    loop(0, AHEAD, lambda q: relay(0, q))
+    spread(1, 1, plane)
+    loop(AHEAD // 2 + 1, AHEAD, lambda q: relay(0, q))
     loop(AHEAD, per, both)
-    for low in range(LANES, rows * n, LANES):
-        turn(low)
-        loop(low // LANES * per, (low // LANES + 1) * per, both)
     relay(1, 0)
+    lows = [(low, c) for low in range(LANES, rows * n, LANES) for c in range(2)]
+    for low, c in lows[: len(lows) // 2]:
+        turn(low, c)
+    relay(1, 1)
+    spread(1, 2, plane)
+    for low, c in lows[len(lows) // 2 :]:
+        turn(low, c)
+    relay(1, 2)
 
     def rest(q):
         spread(1, q, plane)
         relay(1, q)
 
-    loop(1, AHEAD, rest)
-
-    def chunk_rows(q):
-        return pl.ds(pl.multiple_of(q * 2 * wide, 2 * wide), 2 * wide)
+    loop(3, AHEAD, rest)
 
     def absorb(q):
-        loop(1, n, lambda k: polar(q, k).wait_recv())
-        own_polar(q).wait()
+        await_all(mixed.at[:, chunk_rows(q)], p_recv.at[q])
         for c in range(2):
             lesser_raw[:, c, chunk_rows(q), :] = jnp.swapaxes(mixed[c, chunk_rows(q)], 0, 1)
 
     def work(q):
+        @pl.when(q + per < CHUNKS)
+        def _():
+            both(q + per)
+
         @pl.when(q + AHEAD < CHUNKS)
         def _():
             advance(q + AHEAD)
 
         for s in range(2):
-            loop(1, n, lambda k: incoming(s, q, k).wait_recv())
-            own_incoming(s, q).wait()
+            await_all(chunk(targets[s], q), in_recv.at[s, q])
         loop(
             q * group,
             (q + 1) * group,
@@ -462,7 +477,11 @@
         lesser_raw[e, 0] = (bare.astype(jnp.float32) + result[:, :width]).astype(jnp.bfloat16)
         lesser_raw[e, 1] = result[:, width:].astype(jnp.bfloat16)
 
-    loop(0, each, screen_one)
+    def screen_some(i):
+        for j in range(UNROLL):
+            screen_one(i * UNROLL + j)
+
+    loop(0, each // UNROLL, screen_some)
 
     def send_screen(q):
         for c in range(2):
@@ -475,14 +494,13 @@
     def settle(q):
         for s in range(2):
             swap(s, q).wait_send()
-            loop(1, n, lambda k: incoming(s, q, k).wait_send())
-        loop(1, n, lambda k: polar(q, k).wait_send())
+            await_all(sent(targets[s], q, n - 1), in_send.at[s, q])
+        await_all(sent(folded, q, n - 1), p_send.at[q])
 
     loop(0, CHUNKS, settle)
 
     def dress(q):
-        loop(1, n, lambda k: screened(q, k).wait_recv())
-        own_screened(q).wait()
+        await_all(chunk(other_buf, q), w_recv.at[q])
         loop(
             q * group,
             (q + 1) * group,
@@ -494,7 +512,7 @@
         def send_to(target_half):
             def send_one(j):
                 peer = target_half * side + lax.rem(place.seat + j, side)
-                dressed(q, lax.rem(peer - me + n, n), member).start()
+                dressed(q, lax.rem(peer - me + n, n)).start()
 
             return send_one
 
@@ -506,23 +524,14 @@
 
         @pl.when(jnp.logical_not(at_home))
         def _():
-            dressed(q, 0, member).start()
+            dressed(q, 0).start()
 
         loop(1, side, send_to(half))
 
     loop(0, CHUNKS, dress)
 
     def collect(q):
-        @pl.when(at_home)
-        def _():
-            own_dressed(q).wait()
-
-        def wait_one(sender):
-            @pl.when(jnp.logical_not(jnp.logical_and(at_home, sender == member)))
-            def _():
-                dressed(q, 0, sender).wait_recv()
-
-        loop(0, n, wait_one)
+        await_all(sigma.at[:, chunk_rows(q)], s_recv.at[q])
         for c in range(2):
             lesser_raw[:, c, chunk_rows(q), :] = jnp.swapaxes(sigma[c, chunk_rows(q)], 0, 1)
 
@@ -531,12 +540,15 @@
     result.start()
 
     def finish(q):
-        loop(1, n, lambda k: screened(q, k).wait_send())
-        loop(1, n, lambda k: dressed(q, k, member).wait_send())
+        await_all(sent(other_buf, q, n - 1), w_send.at[q])
+
+        @pl.when(at_home)
+        def _():
+            await_all(sent(folded, q, n - 1), s_send.at[q])
 
         @pl.when(jnp.logical_not(at_home))
         def _():
-            dressed(q, 0, member).wait_send()
+            await_all(sent(folded, q, n), s_send.at[q])
 
     loop(0, CHUNKS, finish)
     result.wait()
@@ -552,7 +564,6 @@
     stage = pltpu.VMEM((3, 2, orbitals // 2, each, width), jnp.bfloat16)
     landing = pltpu.VMEM((2, orbitals, each, width), jnp.bfloat16)
     dma = pltpu.SemaphoreType.DMA
-    pairs = dma((CHUNKS, n))
     return pl.pallas_call(
         functools.partial(gw_kernel, n, count, scale),
         name="iterate",
@@ -562,11 +573,9 @@
         scratch_shapes=[
             by_row, by_row, by_row, by_energy, by_energy, stage, stage,
             landing, landing, landing,
-            dma((2, CHUNKS, n)), dma((2, CHUNKS, n)), dma((2, CHUNKS)),
-            dma((2, CHUNKS)), dma((2, CHUNKS)),
-            pairs, pairs, dma((CHUNKS,)),
-            pairs, pairs, dma((CHUNKS,)),
-            pairs, pairs, dma((CHUNKS,)), dma((2,)),
+            dma((2, CHUNKS)), dma((2, CHUNKS)), dma((2, CHUNKS)), dma((2, CHUNKS)),
+            dma((CHUNKS,)), dma((CHUNKS,)), dma((CHUNKS,)), dma((CHUNKS,)),
+            dma((CHUNKS,)), dma((CHUNKS,)), dma((2,)),
         ],
         compiler_params=pltpu.CompilerParams(
             collective_id=0, has_side_effects=True, vmem_limit_bytes=VMEM_BYTES
@@ -613,7 +622,7 @@
 def per_device(n, biases, g_lesser, g_greater, g_free, coulomb):
     each, _, orbitals, _ = g_lesser.shape
     count = n * each
-    if biases != 2 or n % 2 or each % 16 or orbitals % (n * 16) or LANES % (n // 2 * orbitals // n // CHUNKS):
+    if biases != 2 or n % 2 or each % 16 or orbitals % (n * CHUNKS) or LANES % (orbitals // CHUNKS):
         return plain(g_lesser, g_greater, g_free, coulomb)
     scale = 1.0 / (2 * count * count)
     full = transform_table(count)

time: 368 us -> 352 us (0.957); the launches traced: 362 us -> 350 us
  Pallas kernels: 362 us -> 350 us
    pallas_call x1, Pallas kernels: 351 us -> 339 us  [iterate(): pl.pallas_call(functools.partial(gw_kernel, n, count, scale), name='itera...]
where the time goes in v4:
time: 352 us; the launch traced here: 350 us
  Pallas kernels  350 us (99%)
    pallas_call x1, Pallas kernels, iterate(): pl.pallas_call(functools.partial(gw_kernel, n, count, scale), name='itera...  339 us
    pallas_call x1, Pallas kernels, per_energy(): pl.pallas_call(kernel, name=name, grid=(each // 2,), out_shape=jax.ShapeD...  11.4 us

profile of v4, /device:TPU:15, one launch (start us, length us, event | category | flops | bytes accessed | tf_op | source)
XLA Modules:
  0.0 350.0 jit_solution(11514526959872667057)
XLA Ops:
  0.0 338.7 %iterate.1.sigma = bf16[16,2,256,256]{3,2,1,0:T(8,128)(2,1)} custom-call(bf16[16,2,256,256]{3,2,1,0:T(8,128)(2,1)} %lesser.1, bf16[16,2,256,256]{3,2,1,0:T(8,128)(2,1)} %other.1, bf16[1024,512]{1,0:T(8,128)(2,1)} %constant.9.table, bf16[512,1024]{1,0:T(8,128)(2,1)} %constant.10.table_t, bf16[256,256]{1,0:T(8,128)(2,1)} %volts.1), custom_call_target="tpu_custom_call" | custom-call | tf_op jit(solution)/shard_map/iterate/pallas_call | solution.py:567
  338.7 11.4 %dyson.1 = bf16[16,2,256,256]{3,2,1,0:T(8,128)(2,1)} custom-call(bf16[16,2,256,256]{3,2,1,0:T(8,128)(2,1)} %iterate.1.sigma, bf16[16,2,256,256]{3,2,1,0:T(8,128)(2,1)} %free.1), custom_call_target="tpu_custom_call" | custom-call | flops 4294967296 | bytes 8388608 | tf_op jit(solution)/shard_map/dyson/pallas_call | solution.py:607

commit v5 on v4

--- a/solution.py
+++ b/solution.py
@@ -135,6 +135,7 @@
 
 MESH = pl.DeviceIdType.MESH
 CHUNKS = 16
+BLOCKS = 4
 AHEAD = 6
 BEHIND = 4
 UNROLL = 4
@@ -220,10 +221,10 @@
 
 
 def gw_kernel(
-    n, count, scale, lesser, other, table, table_t, volts, out,
+    n, count, scale, lesser, other, free, table, table_t, volts, out,
     lesser_buf, other_buf, folded, lesser_raw, other_raw, lesser_rows, other_rows,
     mixed, screen, sigma,
-    in_send, in_recv, swap_send, swap_recv, p_send, p_recv, w_send, w_recv, s_send, s_recv, keep,
+    in_send, in_recv, swap_send, swap_recv, p_send, p_recv, w_send, w_recv, s_send, s_recv, keep, finals,
 ):
     place = Place(n)
     me, plane, half, side = place.me, place.plane, place.half, place.side
@@ -457,6 +458,8 @@
 
     loop(0, CHUNKS, work)
     loop(CHUNKS - BEHIND, CHUNKS, absorb)
+    free_copy = pltpu.make_async_copy(free, other_raw, keep.at[1])
+    free_copy.start()
     bare = volts[...]
     width = bare.shape[0]
 
@@ -509,15 +512,15 @@
             ),
         )
 
-        def send_to(target_half):
-            def send_one(j):
-                peer = target_half * side + lax.rem(place.seat + j, side)
-                dressed(q, lax.rem(peer - me + n, n)).start()
-
-            return send_one
-
-        loop(0, side, send_to(1 - half))
-
+        def send_far(j):
+            peer = (1 - half) * side + lax.rem(place.seat + j, side)
+            dressed(q, lax.rem(peer - me + n, n)).start()
+
+        loop(0, side, send_far)
+
+    loop(0, CHUNKS, dress)
+
+    def dress_near(q):
         @pl.when(at_home)
         def _():
             own_dressed(q).start()
@@ -526,18 +529,45 @@
         def _():
             dressed(q, 0).start()
 
-        loop(1, side, send_to(half))
-
-    loop(0, CHUNKS, dress)
+        def send_near(j):
+            peer = half * side + lax.rem(place.seat + j, side)
+            dressed(q, lax.rem(peer - me + n, n)).start()
+
+        loop(1, side, send_near)
+
+    loop(0, CHUNKS, dress_near)
 
     def collect(q):
         await_all(sigma.at[:, chunk_rows(q)], s_recv.at[q])
         for c in range(2):
             lesser_raw[:, c, chunk_rows(q), :] = jnp.swapaxes(sigma[c, chunk_rows(q)], 0, 1)
 
-    loop(0, CHUNKS, collect)
-    result = pltpu.make_async_copy(lesser_raw, out, keep.at[0])
-    result.start()
+    span = width // BLOCKS
+
+    def result(i):
+        block = pl.ds(pl.multiple_of(i * span, span), span)
+        return pltpu.make_async_copy(
+            lesser_raw.at[:, :, block], out.at[:, :, block], finals.at[i]
+        )
+
+    def correct(i):
+        loop(i * (CHUNKS // BLOCKS), (i + 1) * (CHUNKS // BLOCKS), collect)
+        block = pl.ds(pl.multiple_of(i * span, span), span)
+
+        def correct_some(j):
+            for e in range(UNROLL):
+                e = j * UNROLL + e
+                pair = jnp.concatenate([lesser_raw[e, 0, block], lesser_raw[e, 1, block]], axis=0)
+                by_real = dot(pair, other_raw[e, 0])
+                by_imag = dot(pair, other_raw[e, 1])
+                lesser_raw[e, 0, block] = (by_real[:span] - by_imag[span:]).astype(jnp.bfloat16)
+                lesser_raw[e, 1, block] = (by_imag[:span] + by_real[span:]).astype(jnp.bfloat16)
+
+        loop(0, each // UNROLL, correct_some)
+        result(i).start()
+
+    free_copy.wait()
+    loop(0, BLOCKS, correct)
 
     def finish(q):
         await_all(sent(other_buf, q, n - 1), w_send.at[q])
@@ -551,10 +581,10 @@
             await_all(sent(folded, q, n), s_send.at[q])
 
     loop(0, CHUNKS, finish)
-    result.wait()
-
-
-def iterate(n, count, scale, g_lesser, g_greater, table, table_t, coulomb):
+    loop(0, BLOCKS, lambda i: result(i).wait())
+
+
+def iterate(n, count, scale, g_lesser, g_greater, g_free, table, table_t, coulomb):
     each, _, orbitals, width = g_lesser.shape
     rows = orbitals // n
     hbm = pl.BlockSpec(memory_space=pl.ANY)
@@ -568,46 +598,46 @@
         functools.partial(gw_kernel, n, count, scale),
         name="iterate",
         out_shape=jax.ShapeDtypeStruct(g_lesser.shape, jnp.bfloat16),
-        in_specs=[hbm, hbm, vmem, vmem, vmem],
+        in_specs=[hbm, hbm, hbm, vmem, vmem, vmem],
         out_specs=hbm,
         scratch_shapes=[
             by_row, by_row, by_row, by_energy, by_energy, stage, stage,
             landing, landing, landing,
             dma((2, CHUNKS)), dma((2, CHUNKS)), dma((2, CHUNKS)), dma((2, CHUNKS)),
             dma((CHUNKS,)), dma((CHUNKS,)), dma((CHUNKS,)), dma((CHUNKS,)),
-            dma((CHUNKS,)), dma((CHUNKS,)), dma((2,)),
+            dma((CHUNKS,)), dma((CHUNKS,)), dma((2,)), dma((BLOCKS,)),
         ],
         compiler_params=pltpu.CompilerParams(
             collective_id=0, has_side_effects=True, vmem_limit_bytes=VMEM_BYTES
         ),
-    )(g_lesser, g_greater, table, table_t, coulomb)
+    )(g_lesser, g_greater, g_free, table, table_t, coulomb)
 
 
 def dot(left, right):
     return jnp.dot(left, right, preferred_element_type=jnp.float32)
 
 
-def dyson_kernel(sigma, free, out):
-    for e in range(sigma.shape[0]):
-        real, imag = sigma[e, 0], sigma[e, 1]
-        free_real, free_imag = free[e, 0], free[e, 1]
-        right_real = (dot(real, free_real) - dot(imag, free_imag)).astype(jnp.bfloat16)
-        right_imag = (dot(real, free_imag) + dot(imag, free_real)).astype(jnp.bfloat16)
-        out_real = dot(free_real, right_real) - dot(free_imag, right_imag)
-        out_imag = dot(free_real, right_imag) + dot(free_imag, right_real)
-        out[e, 0] = (free_real.astype(jnp.float32) + out_real).astype(jnp.bfloat16)
-        out[e, 1] = (free_imag.astype(jnp.float32) + out_imag).astype(jnp.bfloat16)
+def dyson_kernel(right, free, out):
+    rows = right.shape[2]
+    for e in range(right.shape[0]):
+        pair = free[e].reshape(2 * rows, rows)
+        by_real = dot(pair, right[e, 0])
+        by_imag = dot(pair, right[e, 1])
+        out_real = by_real[:rows] - by_imag[rows:]
+        out_imag = by_imag[:rows] + by_real[rows:]
+        out[e, 0] = (free[e, 0].astype(jnp.float32) + out_real).astype(jnp.bfloat16)
+        out[e, 1] = (free[e, 1].astype(jnp.float32) + out_imag).astype(jnp.bfloat16)
 
 
 def per_energy(kernel, name, matrices, others):
     each, two, rows, width = matrices.shape
-    block = pl.BlockSpec((2, two, rows, width), lambda i: (i, 0, 0, 0))
+    block = pl.BlockSpec((4, two, rows, width), lambda i: (i, 0, 0, 0))
     specs = [block if other.ndim == 4 else pl.BlockSpec(memory_space=pltpu.VMEM) for other in others]
-    products = 6 if name == "screen" else 8
+    products = 4
     return pl.pallas_call(
         kernel,
         name=name,
-        grid=(each // 2,),
+        grid=(each // 4,),
         out_shape=jax.ShapeDtypeStruct(matrices.shape, jnp.bfloat16),
         in_specs=[block] + specs,
         out_specs=block,
@@ -628,8 +658,8 @@
     full = transform_table(count)
     table = jnp.asarray(full).astype(jnp.bfloat16)
     table_t = jnp.asarray(full.T).astype(jnp.bfloat16)
-    sigma = iterate(n, count, scale, g_lesser, g_greater, table, table_t, coulomb)
-    return per_energy(dyson_kernel, "dyson", sigma, (g_free,))
+    right = iterate(n, count, scale, g_lesser, g_greater, g_free, table, table_t, coulomb)
+    return per_energy(dyson_kernel, "dyson", right, (g_free,))
 
 
 def solution(mesh):

time: 352 us -> 347 us (0.986)
  Pallas kernels: 350 us -> 346 us
    pallas_call x1, Pallas kernels: 11.4 us -> 7 us  [per_energy(): pl.pallas_call(kernel, name=name, grid=(each // 4,), out_shape=jax.ShapeD...]
where the time goes in v5:
time: 347 us; the launch traced here: 346 us
  Pallas kernels  346 us (100%)
    pallas_call x1, Pallas kernels, iterate(): pl.pallas_call(functools.partial(gw_kernel, n, count, scale), name='itera...  339 us
    pallas_call x1, Pallas kernels, per_energy(): pl.pallas_call(kernel, name=name, grid=(each // 4,), out_shape=jax.ShapeD...  7 us

profile of v5, /device:TPU:15, one launch (start us, length us, event | category | flops | bytes accessed | tf_op | source)
XLA Modules:
  0.0 346.1 jit_solution(12996311312923252629)
XLA Ops:
  0.0 339.1 %iterate.1.right = bf16[16,2,256,256]{3,2,1,0:T(8,128)(2,1)} custom-call(bf16[16,2,256,256]{3,2,1,0:T(8,128)(2,1)} %lesser.1, bf16[16,2,256,256]{3,2,1,0:T(8,128)(2,1)} %other.1, bf16[16,2,256,256]{3,2,1,0:T(8,128)(2,1)} %free.3, bf16[1024,512]{1,0:T(8,128)(2,1)} %constant.9.table, bf16[512,1024]{1,0:T(8,128)(2,1)} %constant.10.table_t, bf16[256,256]{1,0:T(8,128)(2,1)} %volts.1), custom_call_target="tpu_custom_call" | custom-call | tf_op jit(solution)/shard_map/iterate/pallas_call | solution.py:597
  339.1 7.0 %dyson.1 = bf16[16,2,256,256]{3,2,1,0:T(8,128)(2,1)} custom-call(bf16[16,2,256,256]{3,2,1,0:T(8,128)(2,1)} %iterate.1.right, bf16[16,2,256,256]{3,2,1,0:T(8,128)(2,1)} %free.3), custom_call_target="tpu_custom_call" | custom-call | flops 2147483648 | bytes 8388608 | tf_op jit(solution)/shard_map/dyson/pallas_call | solution.py:637
